TPU v7x, 32 devices: a whole 2x2x4 slice. The times are simulated.
32 devices in a mesh: rows: 16 (over z, y, x), tm: 2 (over core).
Axes of the slice: x: 2, y: 2, z: 4, core: 2. Of those that a mesh axis runs over, the one named last changes fastest.
Arguments:
- video: bfloat16 [8, 64, 96, 192], P('tm', 'rows'), may hold values from -6 to 6
- gains: float32 [4, 192], replicated, may hold values from 0.1 to 1.9
- kernels: bfloat16 [4, 3, 3, 3, 192, 192], replicated, may hold values from -0.078125 to 0.078125
Outputs:
- encoded: bfloat16 [8, 64, 96, 192], P('tm', 'rows')
All inputs are finite; a program needn't handle non-finite values.
Results may differ from a plain program's by a relative error of at most 0.0065.
Values may be sent and summed in bfloat16 or wider, within the bound.
No kernel may reach another device: no remote copies, remote signals or barrier semaphores. Data moves between devices by JAX's collectives and lax.ppermute only.
A program may use at most 128 MiB of HBM per device.

v0:
```python
import functools

import jax
import jax.numpy as jnp
from jax import lax
from jax.experimental import pallas as pl
from jax.experimental.pallas import tpu as pltpu
from jax.sharding import PartitionSpec as P

AXES = ("rows", "tm")
EPS = 1e-06
LANES = 128


def activate(x, gain):
    scale = lax.rsqrt(jnp.sum(x * x, axis=-1, keepdims=True) / x.shape[-1] + EPS)
    y = x * scale * gain
    return y / (1.0 + jnp.exp(-y))


class Shape:
    def __init__(self, width, frames, channels):
        self.width, self.frames, self.channels = width, frames, channels
        self.tile = 2 * frames
        self.size = width * frames
        self.rest = channels - LANES
        self.payload = self.size + self.size // 2
        self.chunk = next(m for m in (256, 128, 64, 32, 16) if self.size % m == 0)


def unpack(ref, start, m, sh):
    half = sh.size // 2
    a = ref[start : start + m, :]
    low = start < half
    b = ref[sh.size + start - (0 if low else half) : sh.size + start - (0 if low else half) + m, :]
    b = b[:, : sh.rest] if low else b[:, sh.rest :]
    return a.astype(jnp.float32), b.astype(jnp.float32)


def build(ref, prev, s_ref, c_ref, sh):
    m = sh.tile * 8
    f, tile, n = sh.frames, sh.tile, sh.size
    edges = []
    for start in range(0, n, m):
        parts = []
        for j, x in enumerate(unpack(ref, start, m, sh)):
            x3 = x.reshape(m // f, f, x.shape[-1])
            t = lax.broadcasted_iota(jnp.int32, x3.shape, 1)
            if prev is None:
                p3 = None
            else:
                p3 = unpack(prev, start, m, sh)[j].reshape(x3.shape)
            shifted = [x]
            for step in (1, 2):
                past = jnp.zeros_like(x3) if p3 is None else pltpu.roll(p3, step, 1)
                shifted.append(jnp.where(t >= step, pltpu.roll(x3, step, 1), past).reshape(x.shape))
            parts.append(shifted)
        (a2, a1, a0), (b2, b1, b0) = parts
        whole = jnp.concatenate([a0, a1, a2, jnp.concatenate([b0, b1], axis=1)], axis=1)
        o = tile + start
        s_ref[o : o + m, :] = whole.astype(s_ref.dtype)
        b2h = b2.astype(c_ref.dtype)
        c_ref[o + tile : o + tile + m, : sh.rest] = b2h
        c_ref[o : o + m, sh.rest : 2 * sh.rest] = b2h
        c_ref[o - tile : o - tile + m, 2 * sh.rest :] = b2h
        if start == 0:
            edges.append((whole[f : 2 * f], b2[f : 2 * f]))
        if start + m == n:
            edges.append((whole[m - 2 * f : m - f], b2[m - 2 * f : m - f]))
    (first_s, first_b), (last_s, last_b) = edges
    pad = lambda v: jnp.zeros_like(v)
    s_ref[0:tile, :] = jnp.concatenate([pad(last_s), last_s], axis=0).astype(s_ref.dtype)
    s_ref[tile + n : 2 * tile + n, :] = jnp.concatenate([first_s, pad(first_s)], axis=0).astype(s_ref.dtype)
    c_ref[tile : 2 * tile, : sh.rest] = jnp.concatenate([pad(last_b), last_b], axis=0).astype(c_ref.dtype)
    c_ref[n : n + tile, 2 * sh.rest :] = jnp.concatenate([first_b, pad(first_b)], axis=0).astype(c_ref.dtype)


def taps(s_ref, c_ref, w, base, sh):
    m, total = sh.chunk, None
    for dq in range(3):
        lhs = s_ref[pl.ds(pl.multiple_of(base + sh.tile * dq, sh.tile), m), :]
        k = [w(dt, dq) for dt in range(3)]
        rhs = jnp.concatenate([v[:LANES] for v in k] + [v[LANES:] for v in k[:2]], axis=0)
        part = jnp.dot(lhs, rhs, preferred_element_type=jnp.float32)
        total = part if total is None else total + part
    lhs = c_ref[pl.ds(pl.multiple_of(base + sh.tile, sh.tile), m), :]
    rhs = jnp.concatenate([w(2, dq)[LANES:] for dq in range(3)], axis=0)
    return total + jnp.dot(lhs, rhs, preferred_element_type=jnp.float32)


def finish(acc, base, refs, sh, second, last):
    m = sh.chunk
    here = pl.ds(base, m)
    if second:
        acc = (acc + refs["residual"][here, :].astype(jnp.float32)).astype(jnp.bfloat16)
        refs["hidden"][here, :] = acc
        acc = acc.astype(jnp.float32)
    if not last:
        refs["act"][here, :] = activate(acc, refs["gain"][...])


def pack(act_ref, out_ref, sh):
    n, half = sh.size, sh.size // 2
    out_ref[0:n, :] = act_ref[:, :LANES].astype(out_ref.dtype)
    out_ref[n:, :] = jnp.concatenate([act_ref[:half, LANES:], act_ref[half:, LANES:]], axis=1).astype(out_ref.dtype)


def scratch(rows, sh):
    return [pltpu.VMEM((sh.size + 2 * sh.tile, 4 * LANES), jnp.bfloat16) for _ in range(rows)] + [
        pltpu.VMEM((sh.size + 2 * sh.tile, 3 * sh.rest), jnp.bfloat16) for _ in range(rows)
    ]


def conv_call(kind, layer, core, rows, prevs, kernels, gains, residual, partial, sh):
    second, last = layer % 2 == 1, layer == kernels.shape[0] - 1
    local = kind == "local"
    n, ch = sh.size, sh.channels
    full = lambda x: pl.BlockSpec(x.shape, lambda i, c: (0,) * x.ndim)
    ins, specs, names = [], [], []

    def add(name, value, spec=None):
        ins.append(value)
        specs.append(full(value) if spec is None else spec)
        names.append(name)

    for j, row in enumerate(rows):
        add(f"row{j}", row)
    if prevs is not None:
        for j, row in enumerate(prevs):
            add(f"prev{j}", row)
    if local:
        add("w", kernels, pl.BlockSpec((1, 3, 3, 3, ch, ch), lambda i, c: (layer, 0, 0, 0, 0, 0)))
    else:
        add("w", kernels, pl.BlockSpec((1, 3, 1, 3, ch, ch), lambda i, c: (layer, 0, 2 * c[0], 0, 0, 0)))
        add("partial", partial)
    if not last:
        add("gain", gains[layer + 1][None, :])
    if second:
        add("residual", residual)
    outs, out_names = [], []
    if local:
        outs.append(jax.ShapeDtypeStruct((n, ch), jnp.float32))
        out_names.append("rest")
    if second:
        outs.append(jax.ShapeDtypeStruct((n, ch), jnp.bfloat16))
        out_names.append("hidden")
    if not last:
        outs.append(jax.ShapeDtypeStruct((sh.payload, LANES), jnp.bfloat16))
        out_names.append("packed")
    scratches = scratch(len(rows), sh) + [pltpu.VMEM((n, ch), jnp.float32)]

    def kernel(core_ref, *refs):
        named = dict(zip(names + out_names, refs))
        s = refs[len(names) + len(out_names) :]
        k = len(rows)
        for j in range(k):
            build(named[f"row{j}"], named.get(f"prev{j}"), s[j], s[k + j], sh)
        named["act"] = s[2 * k]
        c = core_ref[0]

        def weight(dr):
            if not local:
                return lambda dt, dq: named["w"][0, dt, 0, dq]
            index = jnp.where(c == 0, dr, 2 - dr)
            return lambda dt, dq: named["w"][0, dt, index, dq]

        def step(i, carry):
            base = pl.multiple_of(i * sh.chunk, sh.chunk)
            tap = lambda row, dr: taps(s[row], s[k + row], weight(dr), base, sh)
            if local:
                inner = tap(0, 0) + tap(1, 1) + tap(2, 2)
                finish(inner, base, named, sh, second, last)
                named["rest"][pl.ds(base, sh.chunk), :] = tap(0, 1) + tap(1, 2)
            else:
                finish(named["partial"][pl.ds(base, sh.chunk), :] + tap(0, 0), base, named, sh, second, last)
            return carry

        lax.fori_loop(0, n // sh.chunk, step, 0)
        if not last:
            pack(named["act"], named["packed"], sh)

    flops = 2 * n * 9 * ch * ch * (5 if local else 1)
    got = pl.pallas_call(
        kernel,
        grid_spec=pltpu.PrefetchScalarGridSpec(
            num_scalar_prefetch=1,
            grid=(1,),
            in_specs=specs,
            out_specs=[full(o) for o in outs],
            scratch_shapes=scratches,
        ),
        out_shape=outs,
        name=f"{kind}{layer}",
        cost_estimate=pl.CostEstimate(flops=flops, transcendentals=0, bytes_accessed=4 << 20),
        compiler_params=pltpu.CompilerParams(vmem_limit_bytes=40 << 20),
    )(core, *ins)
    return dict(zip(out_names, got))


def first_call(rows, gain, sh):
    count = len(rows)
    full = lambda x: pl.BlockSpec(x.shape, lambda i: (0,) * x.ndim)

    def kernel(*refs):
        gain_ref, act = refs[count], refs[2 * count + 1]
        for j in range(count):
            def step(i, carry):
                here = pl.ds(pl.multiple_of(i * sh.chunk, sh.chunk), sh.chunk)
                act[here, :] = activate(refs[j][here, :].astype(jnp.float32), gain_ref[...])
                return carry

            lax.fori_loop(0, sh.size // sh.chunk, step, 0)
            pack(act, refs[count + 1 + j], sh)

    outs = [jax.ShapeDtypeStruct((sh.payload, LANES), jnp.bfloat16) for _ in rows]
    return pl.pallas_call(
        kernel,
        grid=(1,),
        in_specs=[full(r) for r in rows] + [full(gain)],
        out_specs=[full(o) for o in outs],
        out_shape=outs,
        scratch_shapes=[pltpu.VMEM((sh.size, sh.channels), jnp.float32)],
        name="first",
    )(*rows, gain)


def body(video, gains, kernels, count, times):
    f, height, width, ch = video.shape
    half = height // 2
    frames = 2 * f
    sh = Shape(width, frames, ch)
    device = lambda r, t: r * times + t
    index = lax.axis_index("tm")
    core = index % 2
    lower = core == 1
    chip = [(device(r, t), device(r, t ^ 1)) for r in range(count) for t in range(times)]
    outer = [(device(r, t), device(r + 1, t - 1)) for r in range(count - 1) for t in range(1, times, 2)]
    outer += [(b, a) for a, b in outer]
    later = [(device(r, t), device(r, t + 2)) for r in range(count) for t in range(times - 2)]

    top, bottom = video[:, :half], video[:, half:][:, ::-1]
    mine = jnp.where(lower, bottom, top)
    theirs = lax.ppermute(jnp.where(lower, top, bottom), AXES, chip)
    early, late = jnp.where(lower, theirs, mine), jnp.where(lower, mine, theirs)
    whole = jnp.concatenate([early, late], axis=0).reshape(frames, half, 2, width // 2, ch)
    hidden = whole.transpose(1, 3, 2, 0, 4).reshape(half, sh.size, ch)
    hidden = [hidden[j] for j in range(half)]

    packed = first_call(hidden, gains[0][None, :], sh)
    scalar = core.astype(jnp.int32)[None]
    before = (lambda rows: [lax.ppermute(row, AXES, later) for row in rows]) if times > 2 else (lambda rows: None)
    for layer in range(kernels.shape[0]):
        far = lax.ppermute(packed[0], AXES, outer)
        near = lax.ppermute(packed[-1], AXES, chip)
        rows = [packed[0], packed[1], near]
        got = conv_call("local", layer, scalar, rows, before(rows), kernels, gains, hidden[1], None, sh)
        rows = [far]
        done = conv_call("outer", layer, scalar, rows, before(rows), kernels, gains, hidden[0], got["rest"], sh)
        if "hidden" in got:
            hidden = [done["hidden"], got["hidden"]]
        if "packed" in got:
            packed = [done["packed"], got["packed"]]

    result = jnp.stack(hidden).reshape(half, width // 2, 2, frames, ch).transpose(3, 0, 2, 1, 4)
    result = result.reshape(frames, half, width, ch)
    keep = jnp.where(lower, result[f:], result[:f])
    give = jnp.where(lower, result[:f], result[f:])
    taken = lax.ppermute(give, AXES, chip)
    top, bottom = jnp.where(lower, taken, keep), jnp.where(lower, keep, taken)
    return jnp.concatenate([top, bottom[:, ::-1]], axis=1)


def solution(mesh):
    inner = functools.partial(body, count=mesh.shape["rows"], times=mesh.shape["tm"])
    specs = P("tm", "rows", None, None)
    return jax.shard_map(inner, mesh=mesh, in_specs=(specs, P(), P()), out_specs=specs, check_vma=False)
```

profile of v0, /device:TPU:21, one launch (start us, length us, event | category | flops | bytes accessed | tf_op | source)
XLA Modules:
  0.0 71.5 jit_solution(17359004513918179956)
XLA Ops:
  0.0 1.0 %slice.40 = bf16[4,2,96,192]{3,2,1,0:T(8,128)(2,1)S(1)} slice(bf16[4,4,96,192]{3,2,1,0:T(8,128)(2,1)} %param.3), slice={[0:4], [2:4], [0:96], [0:192]} | slice | bytes 589824 | tf_op jit(solution)/shard_map/slice | solution.py:241
  1.0 1.1 %broadcast_select_fusion.5 = bf16[4,2,96,192]{3,2,1,0:T(8,128)(2,1)S(1)} fusion(pred[]{:T(512)S(6)} %eq.5, bf16[4,2,96,192]{3,2,1,0:T(8,128)(2,1)S(1)} %slice.40, bf16[4,4,96,192]{3,2,1,0:T(8,128)(2,1)} %param.3), kind=kLoop, calls=%fused_computation.11 | loop fusion | flops 147456 | bytes 884737 | tf_op jit(solution)/shard_map/jit(_where)/select_n | solution.py:243
  2.1 0.7 %collective-permute-start = (bf16[4,2,96,192]{3,2,1,0:T(8,128)(2,1)S(1)}, bf16[4,2,96,192]{3,2,1,0:T(8,128)(2,1)S(1)}, u32[]{:S(2)}, u32[]{:S(2)}) collective-permute-start(bf16[4,2,96,192]{3,2,1,0:T(8,128)(2,1)S(1)} %broadcast_select_fusion.5), channel_id=1, source_target_pairs={{0,1},{1,0},{2,3},{3,2},{4,5},{5,4},{6,7},{7,6},{8,9},{9,8},{10,11... | collective-permute-start | bytes 884744 | tf_op jit(solution)/shard_map/ppermute | solution.py:243
  2.9 1.4 %fusion.1 = (f32[1,192]{1,0:T(1,128)S(1)}, f32[1,192]{1,0:T(1,128)S(1)}, f32[1,192]{1,0:T(1,128)}, f32[1,192]{1,0:T(1,128)S(1)}) fusion(f32[4,192]{1,0:T(4,128)} %param.4), kind=kLoop, calls=%fused_computation.13 | loop fusion | bytes 6144 | tf_op jit(solution)/shard_map/slice | solution.py:137
  4.3 1.2 %broadcast_select_fusion.3 = (bf16[4,2,96,192]{3,2,1,0:T(8,128)(2,1)S(1)}, bf16[4,2,96,192]{3,2,1,0:T(8,128)(2,1)S(1)}) fusion(bf16[4,2,96,192]{3,2,1,0:T(8,128)(2,1)S(1)} %collective-permute-done, pred[]{:T(512)S(6)} %eq.5, bf16[4,4,96,192]{3,2,1,0:T(8,128)(2,1)} %param.3, bf16[4,2,96,192]{3,2,1,0:T(8,128)(2,1)S(1)} %slice.40), kind=kLoop, calls=%fused_computation.9 | loop fusion | flops 442368 | bytes 1474561 | tf_op jit(solution)/shard_map/jit(_where)/select_n | solution.py:244
  5.6 0.4 copy.8
  6.1 0.9 %fusion = (bf16[1,48,2,8,192]{4,3,2,1,0:T(8,128)(2,1)}, bf16[1,48,2,8,192]{4,3,2,1,0:T(8,128)(2,1)}) fusion(bf16[2,48,2,8,192]{4,3,2,1,0:T(8,128)(2,1)S(1)} %bitcast.21), kind=kLoop, calls=%fused_computation.12 | loop fusion | bytes 1179648 | tf_op jit(solution)/shard_map/slice | solution.py:247
  7.0 3.2 %first.1 = (bf16[1152,128]{1,0:T(8,128)(2,1)}, bf16[1152,128]{1,0:T(8,128)(2,1)}) custom-call(bf16[768,192]{1,0:T(8,128)(2,1)} %bitcast.15, bf16[768,192]{1,0:T(8,128)(2,1)} %bitcast.17, f32[1,192]{1,0:T(1,128)} %get-tuple-element.41.refs_2_), custom_call_target="tpu_custom_call" | custom-call | tf_op jit(solution)/shard_map/first/pallas_call | solution.py:216
  10.5 3.2 %collective-permute-start.1 = (bf16[1152,128]{1,0:T(8,128)(2,1)}, bf16[1152,128]{1,0:T(8,128)(2,1)S(1)}, u32[]{:S(2)}, u32[]{:S(2)}) collective-permute-start(bf16[1152,128]{1,0:T(8,128)(2,1)} %get-tuple-element.18.refs_0_), channel_id=1, source_target_pairs={{1,2},{3,4},{5,6},{7,8},{9,10},{11,12},{13,14},{15,16},{17,18},{19... | collective-permute-start | bytes 884744 | tf_op jit(solution)/shard_map/ppermute | solution.py:253
  13.7 4.0 %copy-done = bf16[4,3,3,3,192,192]{5,4,3,2,1,0:T(8,128)(2,1)S(1)} copy-done((bf16[4,3,3,3,192,192]{5,4,3,2,1,0:T(8,128)(2,1)S(1)}, bf16[4,3,3,3,192,192]{5,4,3,2,1,0:T(8,128)(2,1)}, u32[]{:S(2)}) %copy-start) | copy-done | bytes 7962648
  17.7 1.0 %copy-done.4 = bf16[1152,128]{1,0:T(8,128)(2,1)S(1)} copy-done((bf16[1152,128]{1,0:T(8,128)(2,1)S(1)}, bf16[1152,128]{1,0:T(8,128)(2,1)}, u32[]{:S(2)}) %copy-start.4) | copy-done | bytes 294936
  18.7 1.0 %copy-done.5 = bf16[1152,128]{1,0:T(8,128)(2,1)S(1)} copy-done((bf16[1152,128]{1,0:T(8,128)(2,1)S(1)}, bf16[1152,128]{1,0:T(8,128)(2,1)}, u32[]{:S(2)}) %copy-start.5) | copy-done | bytes 294936
  19.6 5.8 %local0.1 = (f32[768,192]{1,0:T(8,128)S(1)}, bf16[1152,128]{1,0:T(8,128)(2,1)S(1)}) custom-call(s32[1]{0:T(128)} %bitcast.core_ref, bf16[1152,128]{1,0:T(8,128)(2,1)S(1)} %copy-done.4, bf16[1152,128]{1,0:T(8,128)(2,1)S(1)} %copy-done.5, bf16[1152,128]{1,0:T(8,128)(2,1)S(1)} %collective-permute-done.2.refs_2_, bf16[4,3,3,3,192,192]{5,4,3,2,1,0:T(8,128)(2,1)S(1)} %copy-done, ...), custom_call_target="tpu_custom_call" | custom-call | flops 2548039680 | bytes 4194304 | tf_op jit(solution)/shard_map/local0/pallas_call | solution.py:183
  25.5 0.3 collective-permute-start.4
  25.8 2.2 %outer0.1.refs_0_ = bf16[1152,128]{1,0:T(8,128)(2,1)S(1)} custom-call(s32[1]{0:T(128)} %bitcast.core_ref, bf16[1152,128]{1,0:T(8,128)(2,1)S(1)} %collective-permute-done.1.refs_0_, bf16[4,3,3,3,192,192]{5,4,3,2,1,0:T(8,128)(2,1)S(1)} %copy-done.1, f32[768,192]{1,0:T(8,128)S(1)} %get-tuple-element.20.refs_2_, f32[1,192]{1,0:T(1,128)S(1)} %get-tuple-element.40.refs_4_.refs_3_), custom_call_target="tpu_custom_call" | custom-call | flops 509607936 | bytes 4194304 | tf_op jit(solution)/shard_map/outer0/pallas_call | solution.py:183
  28.0 3.3 %collective-permute-start.3 = (bf16[1152,128]{1,0:T(8,128)(2,1)S(1)}, bf16[1152,128]{1,0:T(8,128)(2,1)S(1)}, u32[]{:S(2)}, u32[]{:S(2)}) collective-permute-start(bf16[1152,128]{1,0:T(8,128)(2,1)S(1)} %outer0.1.refs_0_), channel_id=1, source_target_pairs={{1,2},{3,4},{5,6},{7,8},{9,10},{11,12},{13,14},{15,16},{17,18},{19... | collective-permute-start | bytes 884744 | tf_op jit(solution)/shard_map/ppermute | solution.py:253
  31.3 5.8 %local1.1 = (f32[768,192]{1,0:T(8,128)S(1)}, bf16[768,192]{1,0:T(8,128)(2,1)S(1)}, bf16[1152,128]{1,0:T(8,128)(2,1)S(1)}) custom-call(s32[1]{0:T(128)} %bitcast.core_ref, bf16[1152,128]{1,0:T(8,128)(2,1)S(1)} %outer0.1.refs_0_, bf16[1152,128]{1,0:T(8,128)(2,1)S(1)} %get-tuple-element.21.refs_1_, bf16[1152,128]{1,0:T(8,128)(2,1)S(1)} %collective-permute-done.4.refs_2_, ...), custom_call_target="tpu_custom_call" | custom-call | flops 2548039680 | bytes 4194304 | tf_op jit(solution)/shard_map/local1/pallas_call | solution.py:183
  37.2 2.3 %collective-permute-done.3.refs_0_ = bf16[1152,128]{1,0:T(8,128)(2,1)S(1)} collective-permute-done((bf16[1152,128]{1,0:T(8,128)(2,1)S(1)}, bf16[1152,128]{1,0:T(8,128)(2,1)S(1)}, u32[]{:S(2)}, u32[]{:S(2)}) %collective-permute-start.3) | collective-permute-done | bytes 294944 | tf_op jit(solution)/shard_map/ppermute | solution.py:253
  39.5 2.2 %outer1.1 = (bf16[768,192]{1,0:T(8,128)(2,1)S(1)}, bf16[1152,128]{1,0:T(8,128)(2,1)S(1)}) custom-call(s32[1]{0:T(128)} %bitcast.core_ref, bf16[1152,128]{1,0:T(8,128)(2,1)S(1)} %collective-permute-done.3.refs_0_, bf16[4,3,3,3,192,192]{5,4,3,2,1,0:T(8,128)(2,1)S(1)} %copy-done.1, f32[768,192]{1,0:T(8,128)S(1)} %get-tuple-element.22.refs_2_, ...), custom_call_target="tpu_custom_call" | custom-call | flops 509607936 | bytes 4194304 | tf_op jit(solution)/shard_map/outer1/pallas_call | solution.py:183
  41.7 2.8 %collective-permute-start.5 = (bf16[1152,128]{1,0:T(8,128)(2,1)S(1)}, bf16[1152,128]{1,0:T(8,128)(2,1)S(1)}, u32[]{:S(2)}, u32[]{:S(2)}) collective-permute-start(bf16[1152,128]{1,0:T(8,128)(2,1)S(1)} %get-tuple-element.23.refs_0_), channel_id=1, source_target_pairs={{1,2},{3,4},{5,6},{7,8},{9,10},{11,12},{13,14},{15,16},{17,18},{19... | collective-permute-start | bytes 884744 | tf_op jit(solution)/shard_map/ppermute | solution.py:253
  44.5 5.8 %local2.1 = (f32[768,192]{1,0:T(8,128)S(1)}, bf16[1152,128]{1,0:T(8,128)(2,1)S(1)}) custom-call(s32[1]{0:T(128)} %bitcast.core_ref, bf16[1152,128]{1,0:T(8,128)(2,1)S(1)} %get-tuple-element.23.refs_0_, bf16[1152,128]{1,0:T(8,128)(2,1)S(1)} %get-tuple-element.24.refs_1_, bf16[1152,128]{1,0:T(8,128)(2,1)S(1)} %collective-permute-done.6.refs_2_, ...), custom_call_target="tpu_custom_call" | custom-call | flops 2548039680 | bytes 4194304 | tf_op jit(solution)/shard_map/local2/pallas_call | solution.py:183
  50.3 0.9 %collective-permute-start.8 = (bf16[1152,128]{1,0:T(8,128)(2,1)S(1)}, bf16[1152,128]{1,0:T(8,128)(2,1)S(1)}, u32[]{:S(2)}, u32[]{:S(2)}) collective-permute-start(bf16[1152,128]{1,0:T(8,128)(2,1)S(1)} %get-tuple-element.26.refs_1_), channel_id=1, source_target_pairs={{0,1},{1,0},{2,3},{3,2},{4,5},{5,4},{6,7},{7,6},{8,9},{9,8},{10,11... | collective-permute-start | bytes 884744 | tf_op jit(solution)/shard_map/ppermute | solution.py:254
  51.3 1.4 %collective-permute-done.5.refs_0_ = bf16[1152,128]{1,0:T(8,128)(2,1)S(1)} collective-permute-done((bf16[1152,128]{1,0:T(8,128)(2,1)S(1)}, bf16[1152,128]{1,0:T(8,128)(2,1)S(1)}, u32[]{:S(2)}, u32[]{:S(2)}) %collective-permute-start.5) | collective-permute-done | bytes 294944 | tf_op jit(solution)/shard_map/ppermute | solution.py:253
  52.7 2.2 %outer2.1.refs_0_ = bf16[1152,128]{1,0:T(8,128)(2,1)S(1)} custom-call(s32[1]{0:T(128)} %bitcast.core_ref, bf16[1152,128]{1,0:T(8,128)(2,1)S(1)} %collective-permute-done.5.refs_0_, bf16[4,3,3,3,192,192]{5,4,3,2,1,0:T(8,128)(2,1)S(1)} %copy-done.1, f32[768,192]{1,0:T(8,128)S(1)} %get-tuple-element.25.refs_2_, f32[1,192]{1,0:T(1,128)S(1)} %get-tuple-element.39.refs_4_.refs_3_), custom_call_target="tpu_custom_call" | custom-call | flops 509607936 | bytes 4194304 | tf_op jit(solution)/shard_map/outer2/pallas_call | solution.py:183
  54.9 2.1 %collective-permute-start.7 = (bf16[1152,128]{1,0:T(8,128)(2,1)S(1)}, bf16[1152,128]{1,0:T(8,128)(2,1)S(1)}, u32[]{:S(2)}, u32[]{:S(2)}) collective-permute-start(bf16[1152,128]{1,0:T(8,128)(2,1)S(1)} %outer2.1.refs_0_), channel_id=1, source_target_pairs={{1,2},{3,4},{5,6},{7,8},{9,10},{11,12},{13,14},{15,16},{17,18},{19... | collective-permute-start | bytes 884744 | tf_op jit(solution)/shard_map/ppermute | solution.py:253
  57.0 5.3 %local3.1 = (f32[768,192]{1,0:T(8,128)S(1)}, bf16[768,192]{1,0:T(8,128)(2,1)S(1)}) custom-call(s32[1]{0:T(128)} %bitcast.core_ref, bf16[1152,128]{1,0:T(8,128)(2,1)S(1)} %outer2.1.refs_0_, bf16[1152,128]{1,0:T(8,128)(2,1)S(1)} %get-tuple-element.26.refs_1_, bf16[1152,128]{1,0:T(8,128)(2,1)S(1)} %collective-permute-done.8.refs_2_, ...), custom_call_target="tpu_custom_call" | custom-call | flops 2548039680 | bytes 4194304 | tf_op jit(solution)/shard_map/local3/pallas_call | solution.py:183
  62.3 2.5 %collective-permute-done.7.refs_0_ = bf16[1152,128]{1,0:T(8,128)(2,1)S(1)} collective-permute-done((bf16[1152,128]{1,0:T(8,128)(2,1)S(1)}, bf16[1152,128]{1,0:T(8,128)(2,1)S(1)}, u32[]{:S(2)}, u32[]{:S(2)}) %collective-permute-start.7) | collective-permute-done | bytes 294944 | tf_op jit(solution)/shard_map/ppermute | solution.py:253
  64.9 1.7 %outer3.1 = bf16[768,192]{1,0:T(8,128)(2,1)S(1)} custom-call(s32[1]{0:T(128)} %bitcast.core_ref, bf16[1152,128]{1,0:T(8,128)(2,1)S(1)} %collective-permute-done.7.refs_0_, bf16[4,3,3,3,192,192]{5,4,3,2,1,0:T(8,128)(2,1)S(1)} %copy-done.1, f32[768,192]{1,0:T(8,128)S(1)} %get-tuple-element.28.refs_2_, bf16[768,192]{1,0:T(8,128)(2,1)S(1)} %get-tuple-element.29.refs_3_), custom_call_target="tpu_custom_call" | custom-call | flops 509607936 | bytes 4194304 | tf_op jit(solution)/shard_map/outer3/pallas_call | solution.py:183
  66.7 0.4 broadcast_select_fusion
  67.2 1.8 %collective-permute-start.9 = (bf16[4,2,96,192]{3,2,1,0:T(8,128)(2,1)S(1)}, bf16[4,2,96,192]{3,2,1,0:T(8,128)(2,1)S(1)}, u32[]{:S(2)}, u32[]{:S(2)}) collective-permute-start(bf16[4,2,96,192]{3,2,1,0:T(8,128)(2,1)S(1)} %bitcast.23), channel_id=1, source_target_pairs={{0,1},{1,0},{2,3},{3,2},{4,5},{5,4},{6,7},{7,6},{8,9},{9,8},{10,11... | collective-permute-start | bytes 884744 | tf_op jit(solution)/shard_map/ppermute | solution.py:268
  69.1 1.3 %collective-permute-done.9 = bf16[4,2,96,192]{3,2,1,0:T(8,128)(2,1)S(1)} collective-permute-done((bf16[4,2,96,192]{3,2,1,0:T(8,128)(2,1)S(1)}, bf16[4,2,96,192]{3,2,1,0:T(8,128)(2,1)S(1)}, u32[]{:S(2)}, u32[]{:S(2)}) %collective-permute-start.9) | collective-permute-done | bytes 294944 | tf_op jit(solution)/shard_map/ppermute | solution.py:268
  70.5 1.0 %pad_maximum_fusion.1 = bf16[4,4,96,192]{3,2,1,0:T(8,128)(2,1)} fusion(bf16[4,2,96,192]{3,2,1,0:T(8,128)(2,1)S(1)} %rev.7, bf16[4,2,96,192]{3,2,1,0:T(8,128)(2,1)S(1)} %get-tuple-element.33), kind=kLoop, calls=%fused_computation.2 | loop fusion | flops 294912 | bytes 1179648 | tf_op jit(solution)/shard_map/concatenate | solution.py:270
  (23 shorter events, 1.0 us)
Async XLA Ops:
  2.1 2.2 %collective-permute-start = (bf16[4,2,96,192]{3,2,1,0:T(8,128)(2,1)S(1)}, bf16[4,2,96,192]{3,2,1,0:T(8,128)(2,1)S(1)}, u32[]{:S(2)}, u32[]{:S(2)}) collective-permute-start(bf16[4,2,96,192]{3,2,1,0:T(8,128)(2,1)S(1)} %broadcast_select_fusion.5), channel_id=1, source_target_pairs={{0,1},{1,0},{2,3},{3,2},{4,5},{5,4},{6,7},{7,6},{8,9},{9,8},{10,11... | collective-permute-start | bytes 884744 | tf_op jit(solution)/shard_map/ppermute | solution.py:243
  10.2 3.5 %collective-permute-start.2 = (bf16[1152,128]{1,0:T(8,128)(2,1)}, bf16[1152,128]{1,0:T(8,128)(2,1)S(1)}, u32[]{:S(2)}, u32[]{:S(2)}) collective-permute-start(bf16[1152,128]{1,0:T(8,128)(2,1)} %get-tuple-element.19.refs_1_), channel_id=1, source_target_pairs={{0,1},{1,0},{2,3},{3,2},{4,5},{5,4},{6,7},{7,6},{8,9},{9,8},{10,11... | collective-permute-start | bytes 884744 | tf_op jit(solution)/shard_map/ppermute | solution.py:254
  10.5 15.3 %collective-permute-start.1 = (bf16[1152,128]{1,0:T(8,128)(2,1)}, bf16[1152,128]{1,0:T(8,128)(2,1)S(1)}, u32[]{:S(2)}, u32[]{:S(2)}) collective-permute-start(bf16[1152,128]{1,0:T(8,128)(2,1)} %get-tuple-element.18.refs_0_), channel_id=1, source_target_pairs={{1,2},{3,4},{5,6},{7,8},{9,10},{11,12},{13,14},{15,16},{17,18},{19... | collective-permute-start | bytes 884744 | tf_op jit(solution)/shard_map/ppermute | solution.py:253
  13.7 4.0 %copy-start = (bf16[4,3,3,3,192,192]{5,4,3,2,1,0:T(8,128)(2,1)S(1)}, bf16[4,3,3,3,192,192]{5,4,3,2,1,0:T(8,128)(2,1)}, u32[]{:S(2)}) copy-start(bf16[4,3,3,3,192,192]{5,4,3,2,1,0:T(8,128)(2,1)} %refs_1_.7) | copy-start | bytes 23887876
  17.7 1.0 %copy-start.4 = (bf16[1152,128]{1,0:T(8,128)(2,1)S(1)}, bf16[1152,128]{1,0:T(8,128)(2,1)}, u32[]{:S(2)}) copy-start(bf16[1152,128]{1,0:T(8,128)(2,1)} %get-tuple-element.18.refs_0_) | copy-start | bytes 884740
  18.7 1.0 %copy-start.5 = (bf16[1152,128]{1,0:T(8,128)(2,1)S(1)}, bf16[1152,128]{1,0:T(8,128)(2,1)}, u32[]{:S(2)}) copy-start(bf16[1152,128]{1,0:T(8,128)(2,1)} %get-tuple-element.19.refs_1_) | copy-start | bytes 884740
  19.6 6.1 %copy-start.1 = (bf16[4,3,3,3,192,192]{5,4,3,2,1,0:T(8,128)(2,1)S(1)}, bf16[4,3,3,3,192,192]{5,4,3,2,1,0:T(8,128)(2,1)}, u32[]{:S(2)}) copy-start(bf16[4,3,3,3,192,192]{5,4,3,2,1,0:T(8,128)(2,1)} %refs_1_.7) | copy-start | bytes 23887876
  19.6 11.6 %copy-start.3 = (bf16[1,48,2,8,192]{4,3,2,1,0:T(8,128)(2,1)S(1)}, bf16[1,48,2,8,192]{4,3,2,1,0:T(8,128)(2,1)}, u32[]{:S(2)}) copy-start(bf16[1,48,2,8,192]{4,3,2,1,0:T(8,128)(2,1)} %get-tuple-element.37) | copy-start | bytes 884740
  25.5 5.8 %collective-permute-start.4 = (bf16[1152,128]{1,0:T(8,128)(2,1)S(1)}, bf16[1152,128]{1,0:T(8,128)(2,1)S(1)}, u32[]{:S(2)}, u32[]{:S(2)}) collective-permute-start(bf16[1152,128]{1,0:T(8,128)(2,1)S(1)} %get-tuple-element.21.refs_1_), channel_id=1, source_target_pairs={{0,1},{1,0},{2,3},{3,2},{4,5},{5,4},{6,7},{7,6},{8,9},{9,8},{10,11... | collective-permute-start | bytes 884744 | tf_op jit(solution)/shard_map/ppermute | solution.py:254
  25.8 13.7 %copy-start.2 = (bf16[1,48,2,8,192]{4,3,2,1,0:T(8,128)(2,1)S(1)}, bf16[1,48,2,8,192]{4,3,2,1,0:T(8,128)(2,1)}, u32[]{:S(2)}) copy-start(bf16[1,48,2,8,192]{4,3,2,1,0:T(8,128)(2,1)} %get-tuple-element.38) | copy-start | bytes 884740
  28.0 11.5 %collective-permute-start.3 = (bf16[1152,128]{1,0:T(8,128)(2,1)S(1)}, bf16[1152,128]{1,0:T(8,128)(2,1)S(1)}, u32[]{:S(2)}, u32[]{:S(2)}) collective-permute-start(bf16[1152,128]{1,0:T(8,128)(2,1)S(1)} %outer0.1.refs_0_), channel_id=1, source_target_pairs={{1,2},{3,4},{5,6},{7,8},{9,10},{11,12},{13,14},{15,16},{17,18},{19... | collective-permute-start | bytes 884744 | tf_op jit(solution)/shard_map/ppermute | solution.py:253
  37.1 7.4 %collective-permute-start.6 = (bf16[1152,128]{1,0:T(8,128)(2,1)S(1)}, bf16[1152,128]{1,0:T(8,128)(2,1)S(1)}, u32[]{:S(2)}, u32[]{:S(2)}) collective-permute-start(bf16[1152,128]{1,0:T(8,128)(2,1)S(1)} %get-tuple-element.24.refs_1_), channel_id=1, source_target_pairs={{0,1},{1,0},{2,3},{3,2},{4,5},{5,4},{6,7},{7,6},{8,9},{9,8},{10,11... | collective-permute-start | bytes 884744 | tf_op jit(solution)/shard_map/ppermute | solution.py:254
  41.7 11.0 %collective-permute-start.5 = (bf16[1152,128]{1,0:T(8,128)(2,1)S(1)}, bf16[1152,128]{1,0:T(8,128)(2,1)S(1)}, u32[]{:S(2)}, u32[]{:S(2)}) collective-permute-start(bf16[1152,128]{1,0:T(8,128)(2,1)S(1)} %get-tuple-element.23.refs_0_), channel_id=1, source_target_pairs={{1,2},{3,4},{5,6},{7,8},{9,10},{11,12},{13,14},{15,16},{17,18},{19... | collective-permute-start | bytes 884744 | tf_op jit(solution)/shard_map/ppermute | solution.py:253
  50.3 6.7 %collective-permute-start.8 = (bf16[1152,128]{1,0:T(8,128)(2,1)S(1)}, bf16[1152,128]{1,0:T(8,128)(2,1)S(1)}, u32[]{:S(2)}, u32[]{:S(2)}) collective-permute-start(bf16[1152,128]{1,0:T(8,128)(2,1)S(1)} %get-tuple-element.26.refs_1_), channel_id=1, source_target_pairs={{0,1},{1,0},{2,3},{3,2},{4,5},{5,4},{6,7},{7,6},{8,9},{9,8},{10,11... | collective-permute-start | bytes 884744 | tf_op jit(solution)/shard_map/ppermute | solution.py:254
  54.9 10.0 %collective-permute-start.7 = (bf16[1152,128]{1,0:T(8,128)(2,1)S(1)}, bf16[1152,128]{1,0:T(8,128)(2,1)S(1)}, u32[]{:S(2)}, u32[]{:S(2)}) collective-permute-start(bf16[1152,128]{1,0:T(8,128)(2,1)S(1)} %outer2.1.refs_0_), channel_id=1, source_target_pairs={{1,2},{3,4},{5,6},{7,8},{9,10},{11,12},{13,14},{15,16},{17,18},{19... | collective-permute-start | bytes 884744 | tf_op jit(solution)/shard_map/ppermute | solution.py:253
  67.2 3.1 %collective-permute-start.9 = (bf16[4,2,96,192]{3,2,1,0:T(8,128)(2,1)S(1)}, bf16[4,2,96,192]{3,2,1,0:T(8,128)(2,1)S(1)}, u32[]{:S(2)}, u32[]{:S(2)}) collective-permute-start(bf16[4,2,96,192]{3,2,1,0:T(8,128)(2,1)S(1)} %bitcast.23), channel_id=1, source_target_pairs={{0,1},{1,0},{2,3},{3,2},{4,5},{5,4},{6,7},{7,6},{8,9},{9,8},{10,11... | collective-permute-start | bytes 884744 | tf_op jit(solution)/shard_map/ppermute | solution.py:268
where the time goes:
time: 72 us; the launch traced here: 71.5 us
  Pallas kernels  34.2 us (48%)
  starting transfers between devices  15.5 us (22%)
  local copies, waits for them, and re-layouts  9.92 us (14%)
  waiting for transfers between devices  7.53 us (10%)
  other arithmetic  4.1 us (6%)
    pallas_call x8, Pallas kernels, conv_call(): pl.pallas_call(kernel, grid_spec=pltpu.PrefetchScalarGridSpec(num_scalar_...  31 us
    ppermute x4, starting transfers between devices, body(): far = lax.ppermute(packed[0], AXES, outer)  11.4 us
    ppermute x4, waiting for transfers between devices, body(): far = lax.ppermute(packed[0], AXES, outer)  6.24 us
    unnamed x12, local copies, waits for them, and re-layouts  5.94 us
    pallas_call x1, Pallas kernels, first_call(): pl.pallas_call(kernel, grid=(1,), in_specs=[full(r) for r in rows] + [ful...  3.19 us
    ppermute x1, starting transfers between devices, body(): taken = lax.ppermute(give, AXES, chip)  1.77 us
    ppermute x4, starting transfers between devices, body(): near = lax.ppermute(packed[-1], AXES, chip)  1.64 us
  transfers between devices with their start and end apart: 10, of which 4 were waited for; matrix products, arithmetic and copies ran while one was open for 2% of the time, Pallas kernels for 41%

commit v1 on v0

v1 whole, which is shorter than its diff:
```python
import functools

import jax
import jax.numpy as jnp
from jax import lax
from jax.experimental import pallas as pl
from jax.experimental.pallas import tpu as pltpu
from jax.sharding import PartitionSpec as P

AXES = ("rows", "tm")
EPS = 1e-06
LANES = 128


def activate(x, gain):
    scale = lax.rsqrt(jnp.sum(x * x, axis=-1, keepdims=True) / x.shape[-1] + EPS)
    y = x * scale * (0.5 * gain)
    return y + y * jnp.tanh(y)


class Shape:
    def __init__(self, width, frames, channels):
        self.width, self.frames, self.channels = width, frames, channels
        self.tile = 2 * frames
        self.size = width * frames
        self.rest = channels - LANES
        self.payload = self.size + self.size // 2
        self.chunk = next(m for m in (256, 128, 64, 32, 16) if self.size % m == 0)


def unpack(ref, start, m, sh):
    half = sh.size // 2
    a = ref[start : start + m, :]
    low = start < half
    b = ref[sh.size + start - (0 if low else half) : sh.size + start - (0 if low else half) + m, :]
    b = b[:, : sh.rest] if low else b[:, sh.rest :]
    return a.astype(jnp.float32), b.astype(jnp.float32)


def build(ref, prev, s_ref, c_ref, sh):
    m = sh.tile * 8
    f, tile, n = sh.frames, sh.tile, sh.size
    edges = []
    for start in range(0, n, m):
        parts = []
        for j, x in enumerate(unpack(ref, start, m, sh)):
            x3 = x.reshape(m // f, f, x.shape[-1])
            t = lax.broadcasted_iota(jnp.int32, x3.shape, 1)
            if prev is None:
                p3 = None
            else:
                p3 = unpack(prev, start, m, sh)[j].reshape(x3.shape)
            shifted = [x]
            for step in (1, 2):
                past = jnp.zeros_like(x3) if p3 is None else pltpu.roll(p3, step, 1)
                shifted.append(jnp.where(t >= step, pltpu.roll(x3, step, 1), past).reshape(x.shape))
            parts.append(shifted)
        (a2, a1, a0), (b2, b1, b0) = parts
        whole = jnp.concatenate([a0, a1, a2, jnp.concatenate([b0, b1], axis=1)], axis=1)
        o = tile + start
        s_ref[o : o + m, :] = whole.astype(s_ref.dtype)
        b2h = b2.astype(c_ref.dtype)
        c_ref[o + tile : o + tile + m, : sh.rest] = b2h
        c_ref[o : o + m, sh.rest : 2 * sh.rest] = b2h
        c_ref[o - tile : o - tile + m, 2 * sh.rest :] = b2h
        if start == 0:
            edges.append((whole[f : 2 * f], b2[f : 2 * f]))
        if start + m == n:
            edges.append((whole[m - 2 * f : m - f], b2[m - 2 * f : m - f]))
    (first_s, first_b), (last_s, last_b) = edges
    pad = lambda v: jnp.zeros_like(v)
    s_ref[0:tile, :] = jnp.concatenate([pad(last_s), last_s], axis=0).astype(s_ref.dtype)
    s_ref[tile + n : 2 * tile + n, :] = jnp.concatenate([first_s, pad(first_s)], axis=0).astype(s_ref.dtype)
    c_ref[tile : 2 * tile, : sh.rest] = jnp.concatenate([pad(last_b), last_b], axis=0).astype(c_ref.dtype)
    c_ref[n : n + tile, 2 * sh.rest :] = jnp.concatenate([first_b, pad(first_b)], axis=0).astype(c_ref.dtype)


def taps(s_ref, c_ref, w, base, sh):
    m, total = sh.chunk, None
    for dq in range(3):
        lhs = s_ref[base + sh.tile * dq : base + sh.tile * dq + m, :]
        k = [w(dt, dq) for dt in range(3)]
        rhs = jnp.concatenate([v[:LANES] for v in k] + [v[LANES:] for v in k[:2]], axis=0)
        part = jnp.dot(lhs, rhs, preferred_element_type=jnp.float32)
        total = part if total is None else total + part
    lhs = c_ref[base + sh.tile : base + sh.tile + m, :]
    rhs = jnp.concatenate([w(2, dq)[LANES:] for dq in range(3)], axis=0)
    return total + jnp.dot(lhs, rhs, preferred_element_type=jnp.float32)


def finish(acc, base, refs, sh, second, last):
    m = sh.chunk
    here = slice(base, base + m)
    if second:
        acc = (acc + refs["residual"][here, :].astype(jnp.float32)).astype(jnp.bfloat16)
        if last:
            refs["act"][here, :] = acc.astype(jnp.float32)
            return
        refs["hidden"][here, :] = acc
        acc = acc.astype(jnp.float32)
    refs["act"][here, :] = activate(acc, refs["gain"][...])


def pack(act_ref, out_ref, sh):
    n, half = sh.size, sh.size // 2
    out_ref[0:n, :] = act_ref[:, :LANES].astype(out_ref.dtype)
    out_ref[n:, :] = jnp.concatenate([act_ref[:half, LANES:], act_ref[half:, LANES:]], axis=1).astype(out_ref.dtype)


def unpack_row(act_ref, keep_ref, give_ref, core, sh):
    f, w, ch = sh.frames, sh.width // 2, sh.channels
    step = 16
    for q in range(0, w, step):
        x = act_ref[q * sh.tile : (q + step) * sh.tile, :].reshape(step, 2, f, ch)
        for g in range(2):
            y = jnp.swapaxes(x[:, g], 0, 1)
            low, high = y[: f // 2], y[f // 2 :]
            here = slice(g * w + q, g * w + q + step)
            keep_ref[:, here, :] = jnp.where(core == 0, low, high).astype(keep_ref.dtype)
            give_ref[:, here, :] = jnp.where(core == 0, high, low).astype(give_ref.dtype)


def scratch(rows, sh):
    return [pltpu.VMEM((sh.size + 2 * sh.tile, 4 * LANES), jnp.bfloat16) for _ in range(rows)] + [
        pltpu.VMEM((sh.size + 2 * sh.tile, 3 * sh.rest), jnp.bfloat16) for _ in range(rows)
    ]


def conv_call(kind, layer, core, rows, prevs, weights, kernels, gains, residual, partial, sh):
    second, last = layer % 2 == 1, layer == kernels.shape[0] - 1
    local = kind == "local"
    fetch = local and not last
    n, ch = sh.size, sh.channels
    full = lambda x: pl.BlockSpec(x.shape, lambda i, c: (0,) * x.ndim)
    ins, specs, names = [], [], []

    def add(name, value, spec=None):
        ins.append(value)
        specs.append(full(value) if spec is None else spec)
        names.append(name)

    for j, row in enumerate(rows):
        add(f"row{j}", row)
    if prevs is not None:
        for j, row in enumerate(prevs):
            add(f"prev{j}", row)
    add("w", weights)
    if not local:
        add("partial", partial)
    if not last:
        add("gain", gains[layer + 1][None, :])
    if second:
        add("residual", residual)
    if fetch:
        add("kernels", kernels, pl.BlockSpec(memory_space=pltpu.HBM))
    outs, out_names = [], []

    def give(name, shape, dtype=jnp.bfloat16):
        outs.append(jax.ShapeDtypeStruct(shape, dtype))
        out_names.append(name)

    if local:
        give("rest", (n, ch), jnp.float32)
    if last:
        give("keep", (sh.frames // 2, sh.width, ch))
        give("give", (sh.frames // 2, sh.width, ch))
    else:
        if second:
            give("hidden", (n, ch))
        give("packed", (sh.payload, LANES))
    if fetch:
        give("weights", kernels.shape[1:])
    scratches = scratch(len(rows), sh) + [pltpu.VMEM((n, ch), jnp.float32), pltpu.SemaphoreType.DMA(())]

    def kernel(core_ref, *refs):
        named = dict(zip(names + out_names, refs))
        s = refs[len(names) + len(out_names) :]
        k = len(rows)
        if fetch:
            copy = pltpu.make_async_copy(named["kernels"].at[layer + 1], named["weights"], s[2 * k + 1])
            copy.start()
        for j in range(k):
            build(named[f"row{j}"], named.get(f"prev{j}"), s[j], s[k + j], sh)
        named["act"] = s[2 * k]
        c = core_ref[0]

        def weight(dr):
            index = jnp.where(c == 0, dr, 2 - dr)
            return lambda dt, dq: named["w"][dt, index, dq]

        for base in range(0, n, sh.chunk):
            tap = lambda row, dr: taps(s[row], s[k + row], weight(dr), base, sh)
            if local:
                inner = tap(0, 0) + tap(1, 1) + tap(2, 2)
                finish(inner, base, named, sh, second, last)
                named["rest"][base : base + sh.chunk, :] = tap(0, 1) + tap(1, 2)
            else:
                finish(named["partial"][base : base + sh.chunk, :] + tap(0, 0), base, named, sh, second, last)
        if last:
            unpack_row(named["act"], named["keep"], named["give"], c, sh)
        else:
            pack(named["act"], named["packed"], sh)
        if fetch:
            copy.wait()

    flops = 2 * n * 9 * ch * ch * (5 if local else 1)
    got = pl.pallas_call(
        kernel,
        grid_spec=pltpu.PrefetchScalarGridSpec(
            num_scalar_prefetch=1,
            grid=(1,),
            in_specs=specs,
            out_specs=[full(o) for o in outs],
            scratch_shapes=scratches,
        ),
        out_shape=outs,
        name=f"{kind}{layer}",
        cost_estimate=pl.CostEstimate(flops=flops, transcendentals=0, bytes_accessed=4 << 20),
        compiler_params=pltpu.CompilerParams(vmem_limit_bytes=40 << 20),
    )(core, *ins)
    return dict(zip(out_names, got))


def first_call(u, core, video, theirs, gain, kernels, sh):
    f, height, width, ch = video.shape
    half, fetch = height // 2, kernels is not None
    own_row = lambda i, c: (0, jnp.where(c[0] == 0, u, height - 1 - u), 0, 0)
    their_row = lambda i, c: (0, jnp.where(c[0] == 0, u, half - 1 - u), 0, 0)
    block = (f, 1, width, ch)
    outs = [
        jax.ShapeDtypeStruct((sh.size, ch), jnp.bfloat16),
        jax.ShapeDtypeStruct((sh.payload, LANES), jnp.bfloat16),
    ] + ([jax.ShapeDtypeStruct(kernels.shape[1:], kernels.dtype)] if fetch else [])
    full = lambda x: pl.BlockSpec(x.shape, lambda i, c: (0,) * x.ndim)

    def kernel(core_ref, own, other, gain_ref, *refs):
        if fetch:
            copy = pltpu.make_async_copy(refs[0].at[0], refs[3], refs[5])
            copy.start()
            refs = refs[1:]
        hidden, packed, act = refs[0], refs[1], refs[-2]
        c, w, step = core_ref[0], width // 2, 16
        for q in range(0, w, step):
            groups = []
            for g in range(2):
                here = slice(g * w + q, g * w + q + step)
                a, b = own[:, 0, here, :].astype(jnp.float32), other[:, 0, here, :].astype(jnp.float32)
                x = jnp.concatenate([jnp.where(c == 0, a, b), jnp.where(c == 0, b, a)], axis=0)
                groups.append(jnp.swapaxes(x, 0, 1)[:, None])
            x = jnp.concatenate(groups, axis=1).reshape(step * sh.tile, ch)
            rows = slice(q * sh.tile, (q + step) * sh.tile)
            hidden[rows, :] = x.astype(hidden.dtype)
            act[rows, :] = activate(x, gain_ref[...])
        pack(act, packed, sh)
        if fetch:
            copy.wait()

    got = pl.pallas_call(
        kernel,
        grid_spec=pltpu.PrefetchScalarGridSpec(
            num_scalar_prefetch=1,
            grid=(1,),
            in_specs=[pl.BlockSpec(block, own_row), pl.BlockSpec(block, their_row), full(gain)]
            + ([pl.BlockSpec(memory_space=pltpu.HBM)] if fetch else []),
            out_specs=[full(o) for o in outs],
            scratch_shapes=[pltpu.VMEM((sh.size, ch), jnp.float32), pltpu.SemaphoreType.DMA(())],
        ),
        out_shape=outs,
        name=f"first{u}",
        compiler_params=pltpu.CompilerParams(vmem_limit_bytes=40 << 20),
    )(core, video, theirs, gain, *([kernels] if fetch else []))
    return got


def last_call(core, keeps, takens, video, sh):
    height = video.shape[1]
    count = len(keeps)
    full = lambda x: pl.BlockSpec(x.shape, lambda i, c: (0,) * x.ndim)

    def kernel(core_ref, *refs):
        out, sems = refs[2 * count], refs[2 * count + 1]
        c = core_ref[0]
        copies = []
        for j in range(count):
            for part, upper in ((0, c == 0), (count, c != 0)):
                row = jnp.where(upper, j, height - 1 - j)
                copies.append(pltpu.make_async_copy(refs[part + j], out.at[:, row], sems.at[len(copies)]))
                copies[-1].start()
        for copy in copies:
            copy.wait()

    return pl.pallas_call(
        kernel,
        grid_spec=pltpu.PrefetchScalarGridSpec(
            num_scalar_prefetch=1,
            grid=(1,),
            in_specs=[full(k) for k in keeps + takens],
            out_specs=pl.BlockSpec(memory_space=pltpu.HBM),
            scratch_shapes=[pltpu.SemaphoreType.DMA((2 * count,))],
        ),
        out_shape=jax.ShapeDtypeStruct(video.shape, video.dtype),
        name="last",
    )(core, *keeps, *takens)


def body(video, gains, kernels, count, times):
    f, height, width, ch = video.shape
    half = height // 2
    sh = Shape(width, 2 * f, ch)
    device = lambda r, t: r * times + t
    core = lax.axis_index("tm") % 2
    scalar = core.astype(jnp.int32)[None]
    chip = [(device(r, t), device(r, t ^ 1)) for r in range(count) for t in range(times)]
    outer = [(device(r, t), device(r + 1, t - 1)) for r in range(count - 1) for t in range(1, times, 2)]
    outer += [(b, a) for a, b in outer]
    later = [(device(r, t), device(r, t + 2)) for r in range(count) for t in range(times - 2)]
    before = (lambda rows: [lax.ppermute(row, AXES, later) for row in rows]) if times > 2 else (lambda rows: None)

    give = lax.dynamic_slice_in_dim(video, (1 - core) * half, half, axis=1)
    theirs = lax.ppermute(give, AXES, chip)
    h0, p0, weights = first_call(0, scalar, video, theirs, gains[0][None, :], kernels, sh)
    h1, p1 = first_call(1, scalar, video, theirs, gains[0][None, :], None, sh)
    hidden, packed = [h0, h1], [p0, p1]
    for layer in range(kernels.shape[0]):
        far = lax.ppermute(packed[0], AXES, outer)
        near = lax.ppermute(packed[1], AXES, chip)
        rows = [packed[0], packed[1], near]
        got = conv_call("local", layer, scalar, rows, before(rows), weights, kernels, gains, hidden[1], None, sh)
        rows = [far]
        done = conv_call("outer", layer, scalar, rows, before(rows), weights, kernels, gains, hidden[0], got["rest"], sh)
        if "hidden" in got:
            hidden = [done["hidden"], got["hidden"]]
        if "packed" in got:
            packed, weights = [done["packed"], got["packed"]], got["weights"]

    takens = [lax.ppermute(part["give"], AXES, chip) for part in (done, got)]
    return last_call(scalar, [done["keep"], got["keep"]], takens, video, sh)


def solution(mesh):
    inner = functools.partial(body, count=mesh.shape["rows"], times=mesh.shape["tm"])
    specs = P("tm", "rows", None, None)
    return jax.shard_map(inner, mesh=mesh, in_specs=(specs, P(), P()), out_specs=specs, check_vma=False)
```

time: 72 us -> 62.4 us (0.87)
  local copies, waits for them, and re-layouts: 9.92 us -> 4.35 us
  Pallas kernels: 34.2 us -> 28.7 us
  waiting for transfers between devices: 7.53 us -> 12.3 us
  other arithmetic: 4.1 us -> 0 us
  starting transfers between devices: 15.5 us -> 16.3 us
    pallas_call x8, Pallas kernels: 31 us -> 24.3 us  [conv_call(): pl.pallas_call(kernel, grid_spec=pltpu.PrefetchScalarGridSpec(num_scalar_...]
    ppermute x4, waiting for transfers between devices: 6.24 us -> 10.4 us  [body(): far = lax.ppermute(packed[0], AXES, outer)]
    unnamed x12 -> x10, local copies, waits for them, and re-layouts: 5.94 us -> 2.49 us
    select_n x4 -> x0, other arithmetic: 2.8 us -> none  [the longest x1 1.19 us: body(): jnp.where(lower, theirs, mine)]
    ppermute x6 -> x7, starting transfers between devices: 4.16 us -> 6.71 us  [the longest x4 4.29 us: body(): near = lax.ppermute(packed[1], AXES, chip)]
    slice x2 -> x0, local copies, waits for them, and re-layouts: 1.95 us -> none  [the longest x1 1.02 us: body(): top, bottom = (video[:, :half], video[:, half:][:, ::-1])]
    ppermute x4, starting transfers between devices: 11.4 us -> 9.57 us  [body(): far = lax.ppermute(packed[0], AXES, outer)]
    pallas_call x1 -> x3, Pallas kernels: 3.19 us -> 4.42 us  [the longest x2 2.3 us: first_call(): pl.pallas_call(kernel, grid_spec=pltpu.PrefetchScalarGridSpec(num_scalar_...]
  transfers between devices with their start and end apart: 10 -> 11, of which waited for: 4 -> 7; matrix products, arithmetic and copies ran while one was open for 2% -> 1% of each run, Pallas kernels for 41% -> 40%
where the time goes in v1:
time: 62.4 us; the launch traced here: 62 us
  Pallas kernels  28.7 us (46%)
  starting transfers between devices  16.3 us (26%)
  waiting for transfers between devices  12.3 us (20%)
  local copies, waits for them, and re-layouts  4.35 us (7%)
    pallas_call x8, Pallas kernels, conv_call(): pl.pallas_call(kernel, grid_spec=pltpu.PrefetchScalarGridSpec(num_scalar_...  24.3 us
    ppermute x4, waiting for transfers between devices, body(): far = lax.ppermute(packed[0], AXES, outer)  10.4 us
    ppermute x4, starting transfers between devices, body(): far = lax.ppermute(packed[0], AXES, outer)  9.57 us
    ppermute x4, starting transfers between devices, body(): near = lax.ppermute(packed[1], AXES, chip)  4.29 us
    unnamed x10, local copies, waits for them, and re-layouts  2.49 us
    pallas_call x2, Pallas kernels, first_call(): pl.pallas_call(kernel, grid_spec=pltpu.PrefetchScalarGridSpec(num_scalar_...  2.3 us
    pallas_call x1, Pallas kernels, last_call(): pl.pallas_call(kernel, grid_spec=pltpu.PrefetchScalarGridSpec(num_scalar_...  2.12 us
    ppermute x2, starting transfers between devices, body(): takens = [lax.ppermute(part['give'], AXES, chip) for part in (done, got)]  1.68 us
  transfers between devices with their start and end apart: 11, of which 7 were waited for; matrix products, arithmetic and copies ran while one was open for 1% of the time, Pallas kernels for 40%

profile of v1, /device:TPU:21, one launch (start us, length us, event | category | flops | bytes accessed | tf_op | source)
XLA Modules:
  0.0 62.0 jit_solution(4985621322748833736)
XLA Ops:
  0.0 1.0 %constant_dynamic-slice_fusion = bf16[4,2,96,192]{3,2,1,0:T(8,128)(2,1)S(1)} fusion(bf16[4,4,96,192]{3,2,1,0:T(8,128)(2,1)} %own.3, s32[]{:T(128)S(6)} %select_n.11), kind=kLoop, calls=%fused_computation | loop fusion | bytes 589828 | tf_op jit(solution)/shard_map/dynamic_slice | solution.py:319
  1.0 0.7 %collective-permute-start = (bf16[4,2,96,192]{3,2,1,0:T(8,128)(2,1)S(1)}, bf16[4,2,96,192]{3,2,1,0:T(8,128)(2,1)S(1)}, u32[]{:S(2)}, u32[]{:S(2)}) collective-permute-start(bf16[4,2,96,192]{3,2,1,0:T(8,128)(2,1)S(1)} %constant_dynamic-slice_fusion), channel_id=1, source_target_pairs={{0,1},{1,0},{2,3},{3,2},{4,5},{5,4},{6,7},{7,6},{8,9},{9,8},{10,11... | collective-permute-start | bytes 884744 | tf_op jit(solution)/shard_map/ppermute | solution.py:320
  1.8 0.8 %fusion = (f32[1,192]{1,0:T(1,128)S(1)}, f32[1,192]{1,0:T(1,128)S(1)}, f32[1,192]{1,0:T(1,128)S(1)}, f32[1,192]{1,0:T(1,128)S(1)}) fusion(f32[4,192]{1,0:T(4,128)} %param.4), kind=kLoop, calls=%fused_computation.1 | loop fusion | bytes 6144 | tf_op jit(solution)/shard_map/slice | solution.py:151
  2.6 0.5 collective-permute-done.other
  3.1 1.1 %copy-done = bf16[4,4,96,192]{3,2,1,0:T(8,128)(2,1)S(1)} copy-done((bf16[4,4,96,192]{3,2,1,0:T(8,128)(2,1)S(1)}, bf16[4,4,96,192]{3,2,1,0:T(8,128)(2,1)}, u32[]{:S(2)}) %copy-start) | copy-done | bytes 589848
  4.2 0.5 first1.1
  4.8 0.4 collective-permute-start.2
  5.2 1.8 %first0.1 = (bf16[768,192]{1,0:T(8,128)(2,1)S(1)}, bf16[1152,128]{1,0:T(8,128)(2,1)S(1)}, bf16[3,3,3,192,192]{4,3,2,1,0:T(8,128)(2,1)S(1)}) custom-call(s32[1]{0:T(128)} %bitcast.core_ref, bf16[4,4,96,192]{3,2,1,0:T(8,128)(2,1)S(1)} %copy-done, bf16[4,2,96,192]{3,2,1,0:T(8,128)(2,1)S(1)} %collective-permute-done.other, ...), custom_call_target="tpu_custom_call" | custom-call | tf_op jit(solution)/shard_map/first0/pallas_call | solution.py:258
  7.0 3.1 %collective-permute-start.1 = (bf16[1152,128]{1,0:T(8,128)(2,1)S(1)}, bf16[1152,128]{1,0:T(8,128)(2,1)S(1)}, u32[]{:S(2)}, u32[]{:S(2)}) collective-permute-start(bf16[1152,128]{1,0:T(8,128)(2,1)S(1)} %get-tuple-element.27.refs_0_), channel_id=1, source_target_pairs={{1,2},{3,4},{5,6},{7,8},{9,10},{11,12},{13,14},{15,16},{17,18},{19... | collective-permute-start | bytes 884744 | tf_op jit(solution)/shard_map/ppermute | solution.py:325
  10.2 5.5 %local0.1 = (f32[768,192]{1,0:T(8,128)S(1)}, bf16[1152,128]{1,0:T(8,128)(2,1)S(1)}, bf16[3,3,3,192,192]{4,3,2,1,0:T(8,128)(2,1)S(1)}) custom-call(s32[1]{0:T(128)} %bitcast.core_ref, bf16[1152,128]{1,0:T(8,128)(2,1)S(1)} %get-tuple-element.27.refs_0_, bf16[1152,128]{1,0:T(8,128)(2,1)S(1)} %get-tuple-element.29.refs_1_, ...), custom_call_target="tpu_custom_call" | custom-call | flops 2548039680 | bytes 4194304 | tf_op jit(solution)/shard_map/local0/pallas_call | solution.py:207
  15.6 0.4 collective-permute-start.4
  16.0 2.4 %collective-permute-done.1.refs_0_ = bf16[1152,128]{1,0:T(8,128)(2,1)S(1)} collective-permute-done((bf16[1152,128]{1,0:T(8,128)(2,1)S(1)}, bf16[1152,128]{1,0:T(8,128)(2,1)S(1)}, u32[]{:S(2)}, u32[]{:S(2)}) %collective-permute-start.1) | collective-permute-done | bytes 294944 | tf_op jit(solution)/shard_map/ppermute | solution.py:325
  18.4 1.3 %outer0.1.refs_0_ = bf16[1152,128]{1,0:T(8,128)(2,1)S(1)} custom-call(s32[1]{0:T(128)} %bitcast.core_ref, bf16[1152,128]{1,0:T(8,128)(2,1)S(1)} %collective-permute-done.1.refs_0_, bf16[3,3,3,192,192]{4,3,2,1,0:T(8,128)(2,1)S(1)} %get-tuple-element.28.refs_3_.refs_1_, f32[768,192]{1,0:T(8,128)S(1)} %get-tuple-element.30.refs_2_, ...), custom_call_target="tpu_custom_call" | custom-call | flops 509607936 | bytes 4194304 | tf_op jit(solution)/shard_map/outer0/pallas_call | solution.py:207
  19.7 2.4 %collective-permute-start.3 = (bf16[1152,128]{1,0:T(8,128)(2,1)S(1)}, bf16[1152,128]{1,0:T(8,128)(2,1)S(1)}, u32[]{:S(2)}, u32[]{:S(2)}) collective-permute-start(bf16[1152,128]{1,0:T(8,128)(2,1)S(1)} %outer0.1.refs_0_), channel_id=1, source_target_pairs={{1,2},{3,4},{5,6},{7,8},{9,10},{11,12},{13,14},{15,16},{17,18},{19... | collective-permute-start | bytes 884744 | tf_op jit(solution)/shard_map/ppermute | solution.py:325
  22.2 4.2 %local1.1 = (f32[768,192]{1,0:T(8,128)S(1)}, bf16[768,192]{1,0:T(8,128)(2,1)S(1)}, bf16[1152,128]{1,0:T(8,128)(2,1)S(1)}, bf16[3,3,3,192,192]{4,3,2,1,0:T(8,128)(2,1)S(1)}) custom-call(s32[1]{0:T(128)} %bitcast.core_ref, bf16[1152,128]{1,0:T(8,128)(2,1)S(1)} %outer0.1.refs_0_, bf16[1152,128]{1,0:T(8,128)(2,1)S(1)} %get-tuple-element.32.refs_1_, ...), custom_call_target="tpu_custom_call" | custom-call | flops 2548039680 | bytes 4194304 | tf_op jit(solution)/shard_map/local1/pallas_call | solution.py:207
  26.4 1.3 %collective-permute-start.6 = (bf16[1152,128]{1,0:T(8,128)(2,1)S(1)}, bf16[1152,128]{1,0:T(8,128)(2,1)S(1)}, u32[]{:S(2)}, u32[]{:S(2)}) collective-permute-start(bf16[1152,128]{1,0:T(8,128)(2,1)S(1)} %get-tuple-element.38.refs_1_), channel_id=1, source_target_pairs={{0,1},{1,0},{2,3},{3,2},{4,5},{5,4},{6,7},{7,6},{8,9},{9,8},{10,11... | collective-permute-start | bytes 884744 | tf_op jit(solution)/shard_map/ppermute | solution.py:326
  27.7 2.3 %collective-permute-done.3.refs_0_ = bf16[1152,128]{1,0:T(8,128)(2,1)S(1)} collective-permute-done((bf16[1152,128]{1,0:T(8,128)(2,1)S(1)}, bf16[1152,128]{1,0:T(8,128)(2,1)S(1)}, u32[]{:S(2)}, u32[]{:S(2)}) %collective-permute-start.3) | collective-permute-done | bytes 294944 | tf_op jit(solution)/shard_map/ppermute | solution.py:325
  30.0 1.3 %outer1.1 = (bf16[768,192]{1,0:T(8,128)(2,1)S(1)}, bf16[1152,128]{1,0:T(8,128)(2,1)S(1)}) custom-call(s32[1]{0:T(128)} %bitcast.core_ref, bf16[1152,128]{1,0:T(8,128)(2,1)S(1)} %collective-permute-done.3.refs_0_, bf16[3,3,3,192,192]{4,3,2,1,0:T(8,128)(2,1)S(1)} %get-tuple-element.31.refs_3_.refs_1_, f32[768,192]{1,0:T(8,128)S(1)} %get-tuple-element.34.refs_2_, ...), custom_call_target="tpu_custom_call" | custom-call | flops 509607936 | bytes 4194304 | tf_op jit(solution)/shard_map/outer1/pallas_call | solution.py:207
  31.3 2.1 %collective-permute-start.5 = (bf16[1152,128]{1,0:T(8,128)(2,1)S(1)}, bf16[1152,128]{1,0:T(8,128)(2,1)S(1)}, u32[]{:S(2)}, u32[]{:S(2)}) collective-permute-start(bf16[1152,128]{1,0:T(8,128)(2,1)S(1)} %get-tuple-element.36.refs_0_), channel_id=1, source_target_pairs={{1,2},{3,4},{5,6},{7,8},{9,10},{11,12},{13,14},{15,16},{17,18},{19... | collective-permute-start | bytes 884744 | tf_op jit(solution)/shard_map/ppermute | solution.py:325
  33.5 5.5 %local2.1 = (f32[768,192]{1,0:T(8,128)S(1)}, bf16[1152,128]{1,0:T(8,128)(2,1)S(1)}, bf16[3,3,3,192,192]{4,3,2,1,0:T(8,128)(2,1)S(1)}) custom-call(s32[1]{0:T(128)} %bitcast.core_ref, bf16[1152,128]{1,0:T(8,128)(2,1)S(1)} %get-tuple-element.36.refs_0_, bf16[1152,128]{1,0:T(8,128)(2,1)S(1)} %get-tuple-element.38.refs_1_, ...), custom_call_target="tpu_custom_call" | custom-call | flops 2548039680 | bytes 4194304 | tf_op jit(solution)/shard_map/local2/pallas_call | solution.py:207
  38.9 2.2 %collective-permute-start.8 = (bf16[1152,128]{1,0:T(8,128)(2,1)S(1)}, bf16[1152,128]{1,0:T(8,128)(2,1)S(1)}, u32[]{:S(2)}, u32[]{:S(2)}) collective-permute-start(bf16[1152,128]{1,0:T(8,128)(2,1)S(1)} %get-tuple-element.41.refs_1_), channel_id=1, source_target_pairs={{0,1},{1,0},{2,3},{3,2},{4,5},{5,4},{6,7},{7,6},{8,9},{9,8},{10,11... | collective-permute-start | bytes 884744 | tf_op jit(solution)/shard_map/ppermute | solution.py:326
  41.3 1.3 %outer2.1.refs_0_ = bf16[1152,128]{1,0:T(8,128)(2,1)S(1)} custom-call(s32[1]{0:T(128)} %bitcast.core_ref, bf16[1152,128]{1,0:T(8,128)(2,1)S(1)} %collective-permute-done.5.refs_0_, bf16[3,3,3,192,192]{4,3,2,1,0:T(8,128)(2,1)S(1)} %get-tuple-element.37.refs_3_.refs_1_, f32[768,192]{1,0:T(8,128)S(1)} %get-tuple-element.39.refs_2_, ...), custom_call_target="tpu_custom_call" | custom-call | flops 509607936 | bytes 4194304 | tf_op jit(solution)/shard_map/outer2/pallas_call | solution.py:207
  42.6 1.9 %collective-permute-start.7 = (bf16[1152,128]{1,0:T(8,128)(2,1)S(1)}, bf16[1152,128]{1,0:T(8,128)(2,1)S(1)}, u32[]{:S(2)}, u32[]{:S(2)}) collective-permute-start(bf16[1152,128]{1,0:T(8,128)(2,1)S(1)} %outer2.1.refs_0_), channel_id=1, source_target_pairs={{1,2},{3,4},{5,6},{7,8},{9,10},{11,12},{13,14},{15,16},{17,18},{19... | collective-permute-start | bytes 884744 | tf_op jit(solution)/shard_map/ppermute | solution.py:325
  44.5 4.1 %local3.1 = (f32[768,192]{1,0:T(8,128)S(1)}, bf16[4,96,192]{2,1,0:T(8,128)(2,1)S(1)}, bf16[4,96,192]{2,1,0:T(8,128)(2,1)S(1)}) custom-call(s32[1]{0:T(128)} %bitcast.core_ref, bf16[1152,128]{1,0:T(8,128)(2,1)S(1)} %outer2.1.refs_0_, bf16[1152,128]{1,0:T(8,128)(2,1)S(1)} %get-tuple-element.41.refs_1_, bf16[1152,128]{1,0:T(8,128)(2,1)S(1)} %collective-permute-done.8.refs_2_, ...), custom_call_target="tpu_custom_call" | custom-call | flops 2548039680 | bytes 4194304 | tf_op jit(solution)/shard_map/local3/pallas_call | solution.py:207
  48.6 5.5 %collective-permute-done.7.refs_0_ = bf16[1152,128]{1,0:T(8,128)(2,1)S(1)} collective-permute-done((bf16[1152,128]{1,0:T(8,128)(2,1)S(1)}, bf16[1152,128]{1,0:T(8,128)(2,1)S(1)}, u32[]{:S(2)}, u32[]{:S(2)}) %collective-permute-start.7) | collective-permute-done | bytes 294944 | tf_op jit(solution)/shard_map/ppermute | solution.py:325
  54.1 1.2 %outer3.1 = (bf16[4,96,192]{2,1,0:T(8,128)(2,1)S(1)}, bf16[4,96,192]{2,1,0:T(8,128)(2,1)S(1)}) custom-call(s32[1]{0:T(128)} %bitcast.core_ref, bf16[1152,128]{1,0:T(8,128)(2,1)S(1)} %collective-permute-done.7.refs_0_, bf16[3,3,3,192,192]{4,3,2,1,0:T(8,128)(2,1)S(1)} %get-tuple-element.40.refs_3_.refs_1_, f32[768,192]{1,0:T(8,128)S(1)} %get-tuple-element.43.refs_2_, ...), custom_call_target="tpu_custom_call" | custom-call | flops 509607936 | bytes 4194304 | tf_op jit(solution)/shard_map/outer3/pallas_call | solution.py:207
  55.3 0.7 %copy-done.2 = bf16[4,96,192]{2,1,0:T(8,128)(2,1)} copy-done((bf16[4,96,192]{2,1,0:T(8,128)(2,1)}, bf16[4,96,192]{2,1,0:T(8,128)(2,1)S(1)}, u32[]{:S(2)}) %copy-start.2) | copy-done | bytes 147480
  55.9 1.7 %collective-permute-start.9 = (bf16[4,96,192]{2,1,0:T(8,128)(2,1)S(1)}, bf16[4,96,192]{2,1,0:T(8,128)(2,1)S(1)}, u32[]{:S(2)}, u32[]{:S(2)}) collective-permute-start(bf16[4,96,192]{2,1,0:T(8,128)(2,1)S(1)} %get-tuple-element.47), channel_id=1, source_target_pairs={{0,1},{1,0},{2,3},{3,2},{4,5},{5,4},{6,7},{7,6},{8,9},{9,8},{10,11... | collective-permute-start | bytes 442376 | tf_op jit(solution)/shard_map/ppermute | solution.py:336
  57.6 1.1 %collective-permute-done.9.refs_2_ = bf16[4,96,192]{2,1,0:T(8,128)(2,1)S(1)} collective-permute-done((bf16[4,96,192]{2,1,0:T(8,128)(2,1)S(1)}, bf16[4,96,192]{2,1,0:T(8,128)(2,1)S(1)}, u32[]{:S(2)}, u32[]{:S(2)}) %collective-permute-start.9) | collective-permute-done | bytes 147488 | tf_op jit(solution)/shard_map/ppermute | solution.py:336
  58.7 0.4 collective-permute-done.10.refs_3_
  59.3 0.4 copy-done.4
  59.7 2.1 %last.1 = bf16[4,4,96,192]{3,2,1,0:T(8,128)(2,1)} custom-call(s32[1]{0:T(128)} %bitcast.core_ref, bf16[4,96,192]{2,1,0:T(8,128)(2,1)} %copy-done.2, bf16[4,96,192]{2,1,0:T(8,128)(2,1)} %copy-done.1, bf16[4,96,192]{2,1,0:T(8,128)(2,1)} %copy-done.3, bf16[4,96,192]{2,1,0:T(8,128)(2,1)} %copy-done.4), custom_call_target="tpu_custom_call" | custom-call | tf_op jit(solution)/shard_map/last/pallas_call | solution.py:292
  (13 shorter events, 0.5 us)
Async XLA Ops:
  1.0 2.1 %collective-permute-start = (bf16[4,2,96,192]{3,2,1,0:T(8,128)(2,1)S(1)}, bf16[4,2,96,192]{3,2,1,0:T(8,128)(2,1)S(1)}, u32[]{:S(2)}, u32[]{:S(2)}) collective-permute-start(bf16[4,2,96,192]{3,2,1,0:T(8,128)(2,1)S(1)} %constant_dynamic-slice_fusion), channel_id=1, source_target_pairs={{0,1},{1,0},{2,3},{3,2},{4,5},{5,4},{6,7},{7,6},{8,9},{9,8},{10,11... | collective-permute-start | bytes 884744 | tf_op jit(solution)/shard_map/ppermute | solution.py:320
  3.1 1.1 %copy-start = (bf16[4,4,96,192]{3,2,1,0:T(8,128)(2,1)S(1)}, bf16[4,4,96,192]{3,2,1,0:T(8,128)(2,1)}, u32[]{:S(2)}) copy-start(bf16[4,4,96,192]{3,2,1,0:T(8,128)(2,1)} %own.3) | copy-start | bytes 1769476
  4.8 5.4 %collective-permute-start.2 = (bf16[1152,128]{1,0:T(8,128)(2,1)S(1)}, bf16[1152,128]{1,0:T(8,128)(2,1)S(1)}, u32[]{:S(2)}, u32[]{:S(2)}) collective-permute-start(bf16[1152,128]{1,0:T(8,128)(2,1)S(1)} %get-tuple-element.29.refs_1_), channel_id=1, source_target_pairs={{0,1},{1,0},{2,3},{3,2},{4,5},{5,4},{6,7},{7,6},{8,9},{9,8},{10,11... | collective-permute-start | bytes 884744 | tf_op jit(solution)/shard_map/ppermute | solution.py:326
  7.0 11.4 %collective-permute-start.1 = (bf16[1152,128]{1,0:T(8,128)(2,1)S(1)}, bf16[1152,128]{1,0:T(8,128)(2,1)S(1)}, u32[]{:S(2)}, u32[]{:S(2)}) collective-permute-start(bf16[1152,128]{1,0:T(8,128)(2,1)S(1)} %get-tuple-element.27.refs_0_), channel_id=1, source_target_pairs={{1,2},{3,4},{5,6},{7,8},{9,10},{11,12},{13,14},{15,16},{17,18},{19... | collective-permute-start | bytes 884744 | tf_op jit(solution)/shard_map/ppermute | solution.py:325
  15.6 6.5 %collective-permute-start.4 = (bf16[1152,128]{1,0:T(8,128)(2,1)S(1)}, bf16[1152,128]{1,0:T(8,128)(2,1)S(1)}, u32[]{:S(2)}, u32[]{:S(2)}) collective-permute-start(bf16[1152,128]{1,0:T(8,128)(2,1)S(1)} %get-tuple-element.32.refs_1_), channel_id=1, source_target_pairs={{0,1},{1,0},{2,3},{3,2},{4,5},{5,4},{6,7},{7,6},{8,9},{9,8},{10,11... | collective-permute-start | bytes 884744 | tf_op jit(solution)/shard_map/ppermute | solution.py:326
  19.7 10.3 %collective-permute-start.3 = (bf16[1152,128]{1,0:T(8,128)(2,1)S(1)}, bf16[1152,128]{1,0:T(8,128)(2,1)S(1)}, u32[]{:S(2)}, u32[]{:S(2)}) collective-permute-start(bf16[1152,128]{1,0:T(8,128)(2,1)S(1)} %outer0.1.refs_0_), channel_id=1, source_target_pairs={{1,2},{3,4},{5,6},{7,8},{9,10},{11,12},{13,14},{15,16},{17,18},{19... | collective-permute-start | bytes 884744 | tf_op jit(solution)/shard_map/ppermute | solution.py:325
  26.4 7.0 %collective-permute-start.6 = (bf16[1152,128]{1,0:T(8,128)(2,1)S(1)}, bf16[1152,128]{1,0:T(8,128)(2,1)S(1)}, u32[]{:S(2)}, u32[]{:S(2)}) collective-permute-start(bf16[1152,128]{1,0:T(8,128)(2,1)S(1)} %get-tuple-element.38.refs_1_), channel_id=1, source_target_pairs={{0,1},{1,0},{2,3},{3,2},{4,5},{5,4},{6,7},{7,6},{8,9},{9,8},{10,11... | collective-permute-start | bytes 884744 | tf_op jit(solution)/shard_map/ppermute | solution.py:326
  31.3 9.9 %collective-permute-start.5 = (bf16[1152,128]{1,0:T(8,128)(2,1)S(1)}, bf16[1152,128]{1,0:T(8,128)(2,1)S(1)}, u32[]{:S(2)}, u32[]{:S(2)}) collective-permute-start(bf16[1152,128]{1,0:T(8,128)(2,1)S(1)} %get-tuple-element.36.refs_0_), channel_id=1, source_target_pairs={{1,2},{3,4},{5,6},{7,8},{9,10},{11,12},{13,14},{15,16},{17,18},{19... | collective-permute-start | bytes 884744 | tf_op jit(solution)/shard_map/ppermute | solution.py:325
  38.9 5.6 %collective-permute-start.8 = (bf16[1152,128]{1,0:T(8,128)(2,1)S(1)}, bf16[1152,128]{1,0:T(8,128)(2,1)S(1)}, u32[]{:S(2)}, u32[]{:S(2)}) collective-permute-start(bf16[1152,128]{1,0:T(8,128)(2,1)S(1)} %get-tuple-element.41.refs_1_), channel_id=1, source_target_pairs={{0,1},{1,0},{2,3},{3,2},{4,5},{5,4},{6,7},{7,6},{8,9},{9,8},{10,11... | collective-permute-start | bytes 884744 | tf_op jit(solution)/shard_map/ppermute | solution.py:326
  42.6 11.5 %collective-permute-start.7 = (bf16[1152,128]{1,0:T(8,128)(2,1)S(1)}, bf16[1152,128]{1,0:T(8,128)(2,1)S(1)}, u32[]{:S(2)}, u32[]{:S(2)}) collective-permute-start(bf16[1152,128]{1,0:T(8,128)(2,1)S(1)} %outer2.1.refs_0_), channel_id=1, source_target_pairs={{1,2},{3,4},{5,6},{7,8},{9,10},{11,12},{13,14},{15,16},{17,18},{19... | collective-permute-start | bytes 884744 | tf_op jit(solution)/shard_map/ppermute | solution.py:325
  48.6 6.6 %copy-start.1 = (bf16[4,96,192]{2,1,0:T(8,128)(2,1)}, bf16[4,96,192]{2,1,0:T(8,128)(2,1)S(1)}, u32[]{:S(2)}) copy-start(bf16[4,96,192]{2,1,0:T(8,128)(2,1)S(1)} %get-tuple-element.46.refs_1_) | copy-start | bytes 442372
  55.2 0.7 %copy-start.2 = (bf16[4,96,192]{2,1,0:T(8,128)(2,1)}, bf16[4,96,192]{2,1,0:T(8,128)(2,1)S(1)}, u32[]{:S(2)}) copy-start(bf16[4,96,192]{2,1,0:T(8,128)(2,1)S(1)} %get-tuple-element.45.refs_0_) | copy-start | bytes 442372
  55.9 2.7 %collective-permute-start.9 = (bf16[4,96,192]{2,1,0:T(8,128)(2,1)S(1)}, bf16[4,96,192]{2,1,0:T(8,128)(2,1)S(1)}, u32[]{:S(2)}, u32[]{:S(2)}) collective-permute-start(bf16[4,96,192]{2,1,0:T(8,128)(2,1)S(1)} %get-tuple-element.47), channel_id=1, source_target_pairs={{0,1},{1,0},{2,3},{3,2},{4,5},{5,4},{6,7},{7,6},{8,9},{9,8},{10,11... | collective-permute-start | bytes 442376 | tf_op jit(solution)/shard_map/ppermute | solution.py:336
  57.6 1.4 %collective-permute-start.10 = (bf16[4,96,192]{2,1,0:T(8,128)(2,1)S(1)}, bf16[4,96,192]{2,1,0:T(8,128)(2,1)S(1)}, u32[]{:S(2)}, u32[]{:S(2)}) collective-permute-start(bf16[4,96,192]{2,1,0:T(8,128)(2,1)S(1)} %get-tuple-element.48), channel_id=1, source_target_pairs={{0,1},{1,0},{2,3},{3,2},{4,5},{5,4},{6,7},{7,6},{8,9},{9,8},{10,11... | collective-permute-start | bytes 442376 | tf_op jit(solution)/shard_map/ppermute | solution.py:336
  58.7 0.7 %copy-start.3 = (bf16[4,96,192]{2,1,0:T(8,128)(2,1)}, bf16[4,96,192]{2,1,0:T(8,128)(2,1)S(1)}, u32[]{:S(2)}) copy-start(bf16[4,96,192]{2,1,0:T(8,128)(2,1)S(1)} %collective-permute-done.9.refs_2_) | copy-start | bytes 442372
  59.0 0.7 %copy-start.4 = (bf16[4,96,192]{2,1,0:T(8,128)(2,1)}, bf16[4,96,192]{2,1,0:T(8,128)(2,1)S(1)}, u32[]{:S(2)}) copy-start(bf16[4,96,192]{2,1,0:T(8,128)(2,1)S(1)} %collective-permute-done.10.refs_3_) | copy-start | bytes 442372

commit v2 on v1

--- a/solution.py
+++ b/solution.py
@@ -88,7 +88,7 @@
     return total + jnp.dot(lhs, rhs, preferred_element_type=jnp.float32)
 
 
-def finish(acc, base, refs, sh, second, last):
+def finish(acc, base, refs, sh, second, last, inside=None):
     m = sh.chunk
     here = slice(base, base + m)
     if second:
@@ -98,7 +98,8 @@
             return
         refs["hidden"][here, :] = acc
         acc = acc.astype(jnp.float32)
-    refs["act"][here, :] = activate(acc, refs["gain"][...])
+    value = activate(acc, refs["gain"][...])
+    refs["act"][here, :] = value if inside is None else value * inside
 
 
 def pack(act_ref, out_ref, sh):
@@ -128,7 +129,8 @@
 
 def conv_call(kind, layer, core, rows, prevs, weights, kernels, gains, residual, partial, sh):
     second, last = layer % 2 == 1, layer == kernels.shape[0] - 1
-    local = kind == "local"
+    local, edge = kind == "local", kind == "edge"
+    ahead = not second and not edge
     fetch = local and not last
     n, ch = sh.size, sh.channels
     full = lambda x: pl.BlockSpec(x.shape, lambda i, c: (0,) * x.ndim)
@@ -144,9 +146,13 @@
     if prevs is not None:
         for j, row in enumerate(prevs):
             add(f"prev{j}", row)
-    add("w", weights)
+    start = weights is None
+    if not start:
+        add("w", weights)
     if not local:
-        add("partial", partial)
+        add("partial", partial[0])
+        if ahead:
+            add("beyond", partial[1])
     if not last:
         add("gain", gains[layer + 1][None, :])
     if second:
@@ -161,6 +167,8 @@
 
     if local:
         give("rest", (n, ch), jnp.float32)
+    if ahead:
+        give("edge", (n, ch), jnp.float32)
     if last:
         give("keep", (sh.frames // 2, sh.width, ch))
         give("give", (sh.frames // 2, sh.width, ch))
@@ -170,32 +178,46 @@
         give("packed", (sh.payload, LANES))
     if fetch:
         give("weights", kernels.shape[1:])
-    scratches = scratch(len(rows), sh) + [pltpu.VMEM((n, ch), jnp.float32), pltpu.SemaphoreType.DMA(())]
+    if start:
+        give("w", kernels.shape[1:])
+    scratches = scratch(len(rows), sh) + [pltpu.VMEM((n, ch), jnp.float32), pltpu.SemaphoreType.DMA((2,))]
 
     def kernel(core_ref, *refs):
         named = dict(zip(names + out_names, refs))
         s = refs[len(names) + len(out_names) :]
         k = len(rows)
+        if start:
+            begin = pltpu.make_async_copy(named["kernels"].at[layer], named["w"], s[2 * k + 1].at[1])
+            begin.start()
         if fetch:
-            copy = pltpu.make_async_copy(named["kernels"].at[layer + 1], named["weights"], s[2 * k + 1])
+            copy = pltpu.make_async_copy(named["kernels"].at[layer + 1], named["weights"], s[2 * k + 1].at[0])
             copy.start()
         for j in range(k):
             build(named[f"row{j}"], named.get(f"prev{j}"), s[j], s[k + j], sh)
+        if start:
+            begin.wait()
         named["act"] = s[2 * k]
-        c = core_ref[0]
+        c = core_ref[0] & 1
 
         def weight(dr):
             index = jnp.where(c == 0, dr, 2 - dr)
             return lambda dt, dq: named["w"][dt, index, dq]
 
         for base in range(0, n, sh.chunk):
+            here = slice(base, base + sh.chunk)
             tap = lambda row, dr: taps(s[row], s[k + row], weight(dr), base, sh)
             if local:
-                inner = tap(0, 0) + tap(1, 1) + tap(2, 2)
-                finish(inner, base, named, sh, second, last)
-                named["rest"][base : base + sh.chunk, :] = tap(0, 1) + tap(1, 2)
+                named["act"][here, :] = tap(0, 0) + tap(1, 1) + tap(2, 2)
+                named["rest"][here, :] = tap(0, 1) + tap(1, 2)
+                if ahead:
+                    named["edge"][here, :] = tap(0, 2)
             else:
-                finish(named["partial"][base : base + sh.chunk, :] + tap(0, 0), base, named, sh, second, last)
+                inside = (core_ref[0] >> 1).astype(jnp.float32) if edge else None
+                finish(named["partial"][here, :] + tap(0, 0), base, named, sh, second, last, inside)
+                if ahead:
+                    named["edge"][here, :] = named["beyond"][here, :] + tap(0, 1)
+        for base in range(0, n if local else 0, sh.chunk):
+            finish(named["act"][base : base + sh.chunk, :], base, named, sh, second, last)
         if last:
             unpack_row(named["act"], named["keep"], named["give"], c, sh)
         else:
@@ -203,7 +225,7 @@
         if fetch:
             copy.wait()
 
-    flops = 2 * n * 9 * ch * ch * (5 if local else 1)
+    flops = 2 * n * 9 * ch * ch * ((5 if local else 1) + ahead)
     got = pl.pallas_call(
         kernel,
         grid_spec=pltpu.PrefetchScalarGridSpec(
@@ -221,11 +243,10 @@
     return dict(zip(out_names, got))
 
 
-def first_call(u, core, video, theirs, gain, kernels, sh):
-    f, height, width, ch = video.shape
-    half, fetch = height // 2, kernels is not None
-    own_row = lambda i, c: (0, jnp.where(c[0] == 0, u, height - 1 - u), 0, 0)
-    their_row = lambda i, c: (0, jnp.where(c[0] == 0, u, half - 1 - u), 0, 0)
+def first_call(u, core, mine, theirs, gain, kernels, sh):
+    f, half, width, ch = mine.shape
+    fetch = kernels is not None
+    row = lambda i, c: (0, jnp.where((c[0] & 1) == 0, u, half - 1 - u), 0, 0)
     block = (f, 1, width, ch)
     outs = [
         jax.ShapeDtypeStruct((sh.size, ch), jnp.bfloat16),
@@ -239,7 +260,7 @@
             copy.start()
             refs = refs[1:]
         hidden, packed, act = refs[0], refs[1], refs[-2]
-        c, w, step = core_ref[0], width // 2, 16
+        c, w, step = core_ref[0] & 1, width // 2, 16
         for q in range(0, w, step):
             groups = []
             for g in range(2):
@@ -260,7 +281,7 @@
         grid_spec=pltpu.PrefetchScalarGridSpec(
             num_scalar_prefetch=1,
             grid=(1,),
-            in_specs=[pl.BlockSpec(block, own_row), pl.BlockSpec(block, their_row), full(gain)]
+            in_specs=[pl.BlockSpec(block, row), pl.BlockSpec(block, row), full(gain)]
             + ([pl.BlockSpec(memory_space=pltpu.HBM)] if fetch else []),
             out_specs=[full(o) for o in outs],
             scratch_shapes=[pltpu.VMEM((sh.size, ch), jnp.float32), pltpu.SemaphoreType.DMA(())],
@@ -268,7 +289,7 @@
         out_shape=outs,
         name=f"first{u}",
         compiler_params=pltpu.CompilerParams(vmem_limit_bytes=40 << 20),
-    )(core, video, theirs, gain, *([kernels] if fetch else []))
+    )(core, mine, theirs, gain, *([kernels] if fetch else []))
     return got
 
 
@@ -279,7 +300,7 @@
 
     def kernel(core_ref, *refs):
         out, sems = refs[2 * count], refs[2 * count + 1]
-        c = core_ref[0]
+        c = core_ref[0] & 1
         copies = []
         for j in range(count):
             for part, upper in ((0, c == 0), (count, c != 0)):
@@ -300,6 +321,7 @@
         ),
         out_shape=jax.ShapeDtypeStruct(video.shape, video.dtype),
         name="last",
+        compiler_params=pltpu.CompilerParams(vmem_limit_bytes=4 << 20),
     )(core, *keeps, *takens)
 
 
@@ -309,7 +331,9 @@
     sh = Shape(width, 2 * f, ch)
     device = lambda r, t: r * times + t
     core = lax.axis_index("tm") % 2
-    scalar = core.astype(jnp.int32)[None]
+    index = lax.axis_index("rows")
+    inside = jnp.where(core == 0, index > 0, index < count - 1)
+    scalar = (core.astype(jnp.int32) + 2 * inside.astype(jnp.int32))[None]
     chip = [(device(r, t), device(r, t ^ 1)) for r in range(count) for t in range(times)]
     outer = [(device(r, t), device(r + 1, t - 1)) for r in range(count - 1) for t in range(1, times, 2)]
     outer += [(b, a) for a, b in outer]
@@ -318,20 +342,28 @@
 
     give = lax.dynamic_slice_in_dim(video, (1 - core) * half, half, axis=1)
     theirs = lax.ppermute(give, AXES, chip)
-    h0, p0, weights = first_call(0, scalar, video, theirs, gains[0][None, :], kernels, sh)
-    h1, p1 = first_call(1, scalar, video, theirs, gains[0][None, :], None, sh)
+    mine = lax.dynamic_slice_in_dim(video, core * half, half, axis=1)
+    gain = gains[0][None, :]
+    h0, p0 = first_call(0, scalar, mine, theirs, gain, None, sh)
+    h1, p1 = first_call(1, scalar, mine, theirs, gain, None, sh)
+    weights = None
     hidden, packed = [h0, h1], [p0, p1]
-    for layer in range(kernels.shape[0]):
-        far = lax.ppermute(packed[0], AXES, outer)
+    for layer in range(0, kernels.shape[0], 2):
+        call = lambda kind, step, rows, weights, residual, partial: conv_call(
+            kind, layer + step, scalar, rows, before(rows), weights, kernels, gains, residual, partial, sh
+        )
+        far = [lax.ppermute(row, AXES, outer) for row in packed]
         near = lax.ppermute(packed[1], AXES, chip)
-        rows = [packed[0], packed[1], near]
-        got = conv_call("local", layer, scalar, rows, before(rows), weights, kernels, gains, hidden[1], None, sh)
-        rows = [far]
-        done = conv_call("outer", layer, scalar, rows, before(rows), weights, kernels, gains, hidden[0], got["rest"], sh)
-        if "hidden" in got:
-            hidden = [done["hidden"], got["hidden"]]
+        a = call("local", 0, packed + [near], weights, None, None)
+        weights = a.get("w", weights)
+        near = lax.ppermute(a["packed"], AXES, chip)
+        b = call("outer", 0, far[:1], weights, None, [a["rest"], a["edge"]])
+        got = call("local", 1, [b["packed"], a["packed"], near], a["weights"], hidden[1], None)
+        c = call("edge", 0, far[1:], weights, None, [b["edge"]])
+        done = call("outer", 1, [c["packed"]], a["weights"], hidden[0], [got["rest"]])
         if "packed" in got:
-            packed, weights = [done["packed"], got["packed"]], got["weights"]
+            hidden, packed = [done["hidden"], got["hidden"]], [done["packed"], got["packed"]]
+            weights = got["weights"]
 
     takens = [lax.ppermute(part["give"], AXES, chip) for part in (done, got)]
     return last_call(scalar, [done["keep"], got["keep"]], takens, video, sh)

time: 62.4 us -> 57.5 us (0.921)
  waiting for transfers between devices: 12.3 us -> 6.38 us
  Pallas kernels: 28.7 us -> 32.1 us
  local copies, waits for them, and re-layouts: 4.35 us -> 2.02 us
    ppermute x4 -> x6, waiting for transfers between devices: 10.4 us -> 4.5 us  [the longest x4 4.5 us: body(): far = [lax.ppermute(row, AXES, outer) for row in packed]]
    pallas_call x8 -> x10, Pallas kernels: 24.3 us -> 30.1 us  [conv_call(): pl.pallas_call(kernel, grid_spec=pltpu.PrefetchScalarGridSpec(num_scalar_...]
    ppermute x4 -> x6, starting transfers between devices: 9.57 us -> 14 us  [the longest x4 12.3 us: body(): far = [lax.ppermute(row, AXES, outer) for row in packed]]
    ppermute x4 -> x2, starting transfers between devices: 4.29 us -> 0.51 us  [body(): near = lax.ppermute(packed[1], AXES, chip)]
    unnamed x10 -> x0, local copies, waits for them, and re-layouts: 2.49 us -> none
    pallas_call x2, Pallas kernels: 2.3 us -> 1.07 us  [first_call(): pl.pallas_call(kernel, grid_spec=pltpu.PrefetchScalarGridSpec(num_scalar_...]
    pallas_call x1, Pallas kernels: 2.12 us -> 0.9 us  [last_call(): pl.pallas_call(kernel, grid_spec=pltpu.PrefetchScalarGridSpec(num_scalar_...]
  transfers between devices with their start and end apart: 11 -> 11, of which waited for: 7 -> 5; matrix products, arithmetic and copies ran while one was open for 1% -> 1% of each run, Pallas kernels for 40% -> 44%
where the time goes in v2:
time: 57.5 us; the launch traced here: 57.2 us
  Pallas kernels  32.1 us (56%)
  starting transfers between devices  16.4 us (29%)
  waiting for transfers between devices  6.38 us (11%)
  local copies, waits for them, and re-layouts  2.02 us (4%)
    pallas_call x10, Pallas kernels, conv_call(): pl.pallas_call(kernel, grid_spec=pltpu.PrefetchScalarGridSpec(num_scalar_...  30.1 us
    ppermute x4, starting transfers between devices, body(): far = [lax.ppermute(row, AXES, outer) for row in packed]  12.3 us
    ppermute x4, waiting for transfers between devices, body(): far = [lax.ppermute(row, AXES, outer) for row in packed]  4.5 us
    ppermute x2, starting transfers between devices, body(): near = lax.ppermute(a['packed'], AXES, chip)  1.73 us
    ppermute x2, waiting for transfers between devices, body(): takens = [lax.ppermute(part['give'], AXES, chip) for part in (done, got)]  1.36 us
    dynamic_slice x1, local copies, waits for them, and re-layouts, body(): give = lax.dynamic_slice_in_dim(video, (1 - core) * half, half, axis=1)  1.18 us
  transfers between devices with their start and end apart: 11, of which 5 were waited for; matrix products, arithmetic and copies ran while one was open for 1% of the time, Pallas kernels for 44%

profile of v2, /device:TPU:21, one launch (start us, length us, event | category | flops | bytes accessed | tf_op | source)
XLA Modules:
  0.0 57.2 jit_solution(10802711512094282246)
XLA Ops:
  0.0 1.2 %constant_dynamic-slice_fusion = (bf16[4,2,96,192]{3,2,1,0:T(8,128)(2,1)S(1)}, bf16[4,2,96,192]{3,2,1,0:T(8,128)(2,1)S(1)}) fusion(bf16[4,4,96,192]{3,2,1,0:T(8,128)(2,1)} %param.3, s32[]{:T(128)S(6)} %select_n.20, s32[]{:T(128)S(6)} %select_n.19), kind=kLoop, calls=%fused_computation | loop fusion | bytes 1179656 | tf_op jit(solution)/shard_map/dynamic_slice | solution.py:343
  1.2 0.7 %collective-permute-start = (bf16[4,2,96,192]{3,2,1,0:T(8,128)(2,1)S(1)}, bf16[4,2,96,192]{3,2,1,0:T(8,128)(2,1)S(1)}, u32[]{:S(2)}, u32[]{:S(2)}) collective-permute-start(bf16[4,2,96,192]{3,2,1,0:T(8,128)(2,1)S(1)} %get-tuple-element.61), channel_id=1, source_target_pairs={{0,1},{1,0},{2,3},{3,2},{4,5},{5,4},{6,7},{7,6},{8,9},{9,8},{10,11... | collective-permute-start | bytes 884744 | tf_op jit(solution)/shard_map/ppermute | solution.py:344
  1.9 0.8 %fusion = (f32[1,192]{1,0:T(1,128)S(1)}, f32[1,192]{1,0:T(1,128)S(1)}, f32[1,192]{1,0:T(1,128)S(1)}, f32[1,192]{1,0:T(1,128)S(1)}) fusion(f32[4,192]{1,0:T(4,128)} %param.4), kind=kLoop, calls=%fused_computation.2 | loop fusion | bytes 6144 | tf_op jit(solution)/shard_map/slice | solution.py:157
  2.8 0.5 collective-permute-done.other
  3.3 0.5 first1.1
  3.8 0.4 collective-permute-start.2
  4.3 0.5 first0.1
  4.8 3.1 %collective-permute-start.1 = (bf16[1152,128]{1,0:T(8,128)(2,1)S(1)}, bf16[1152,128]{1,0:T(8,128)(2,1)S(1)}, u32[]{:S(2)}, u32[]{:S(2)}) collective-permute-start(bf16[1152,128]{1,0:T(8,128)(2,1)S(1)} %get-tuple-element.33.refs_0_), channel_id=1, source_target_pairs={{1,2},{3,4},{5,6},{7,8},{9,10},{11,12},{13,14},{15,16},{17,18},{19... | collective-permute-start | bytes 884744 | tf_op jit(solution)/shard_map/ppermute | solution.py:355
  7.9 0.0 collective-permute-done.2.refs_2_
  8.0 6.6 %local0.1 = (f32[768,192]{1,0:T(8,128)S(1)}, f32[768,192]{1,0:T(8,128)S(1)}, bf16[1152,128]{1,0:T(8,128)(2,1)S(1)}, bf16[3,3,3,192,192]{4,3,2,1,0:T(8,128)(2,1)S(1)}, bf16[3,3,3,192,192]{4,3,2,1,0:T(8,128)(2,1)S(1)}) custom-call(s32[1]{0:T(128)} %bitcast.core_ref, bf16[1152,128]{1,0:T(8,128)(2,1)S(1)} %get-tuple-element.33.refs_0_, ...), custom_call_target="tpu_custom_call" | custom-call | flops 3057647616 | bytes 4194304 | tf_op jit(solution)/shard_map/local0/pallas_call | solution.py:229
  14.5 0.4 collective-permute-start.3
  14.9 3.4 %collective-permute-start.5 = (bf16[1152,128]{1,0:T(8,128)(2,1)S(1)}, bf16[1152,128]{1,0:T(8,128)(2,1)S(1)}, u32[]{:S(2)}, u32[]{:S(2)}) collective-permute-start(bf16[1152,128]{1,0:T(8,128)(2,1)S(1)} %get-tuple-element.34.refs_1_), channel_id=1, source_target_pairs={{1,2},{3,4},{5,6},{7,8},{9,10},{11,12},{13,14},{15,16},{17,18},{19... | collective-permute-start | bytes 884744 | tf_op jit(solution)/shard_map/ppermute | solution.py:355
  18.3 1.8 %outer0.1 = (f32[768,192]{1,0:T(8,128)S(1)}, bf16[1152,128]{1,0:T(8,128)(2,1)S(1)}) custom-call(s32[1]{0:T(128)} %bitcast.core_ref, bf16[1152,128]{1,0:T(8,128)(2,1)S(1)} %collective-permute-done.1.refs_0_, bf16[3,3,3,192,192]{4,3,2,1,0:T(8,128)(2,1)S(1)} %get-tuple-element.35.refs_1_, f32[768,192]{1,0:T(8,128)S(1)} %get-tuple-element.36.refs_2_, ...), custom_call_target="tpu_custom_call" | custom-call | flops 1019215872 | bytes 4194304 | tf_op jit(solution)/shard_map/outer0/pallas_call | solution.py:229
  20.2 4.3 %local1.1 = (f32[768,192]{1,0:T(8,128)S(1)}, bf16[768,192]{1,0:T(8,128)(2,1)S(1)}, bf16[1152,128]{1,0:T(8,128)(2,1)S(1)}, bf16[3,3,3,192,192]{4,3,2,1,0:T(8,128)(2,1)S(1)}) custom-call(s32[1]{0:T(128)} %bitcast.core_ref, bf16[1152,128]{1,0:T(8,128)(2,1)S(1)} %get-tuple-element.38.refs_0_, bf16[1152,128]{1,0:T(8,128)(2,1)S(1)} %get-tuple-element.39.refs_1_, ...), custom_call_target="tpu_custom_call" | custom-call | flops 2548039680 | bytes 4194304 | tf_op jit(solution)/shard_map/local1/pallas_call | solution.py:229
  24.5 0.1 collective-permute-start.7
  24.6 1.8 %collective-permute-done.5.refs_0_ = bf16[1152,128]{1,0:T(8,128)(2,1)S(1)} collective-permute-done((bf16[1152,128]{1,0:T(8,128)(2,1)S(1)}, bf16[1152,128]{1,0:T(8,128)(2,1)S(1)}, u32[]{:S(2)}, u32[]{:S(2)}) %collective-permute-start.5) | collective-permute-done | bytes 294944 | tf_op jit(solution)/shard_map/ppermute | solution.py:355
  26.4 1.3 %edge0.1.refs_0_ = bf16[1152,128]{1,0:T(8,128)(2,1)S(1)} custom-call(s32[1]{0:T(128)} %bitcast.core_ref, bf16[1152,128]{1,0:T(8,128)(2,1)S(1)} %collective-permute-done.5.refs_0_, bf16[3,3,3,192,192]{4,3,2,1,0:T(8,128)(2,1)S(1)} %get-tuple-element.35.refs_1_, f32[768,192]{1,0:T(8,128)S(1)} %get-tuple-element.44.refs_2_, ...), custom_call_target="tpu_custom_call" | custom-call | flops 509607936 | bytes 4194304 | tf_op jit(solution)/shard_map/edge0/pallas_call | solution.py:229
  27.7 2.8 %collective-permute-start.4 = (bf16[1152,128]{1,0:T(8,128)(2,1)S(1)}, bf16[1152,128]{1,0:T(8,128)(2,1)S(1)}, u32[]{:S(2)}, u32[]{:S(2)}) collective-permute-start(bf16[1152,128]{1,0:T(8,128)(2,1)S(1)} %get-tuple-element.42.refs_1_), channel_id=1, source_target_pairs={{1,2},{3,4},{5,6},{7,8},{9,10},{11,12},{13,14},{15,16},{17,18},{19... | collective-permute-start | bytes 884744 | tf_op jit(solution)/shard_map/ppermute | solution.py:355
  30.5 1.3 %outer1.1 = (bf16[768,192]{1,0:T(8,128)(2,1)S(1)}, bf16[1152,128]{1,0:T(8,128)(2,1)S(1)}) custom-call(s32[1]{0:T(128)} %bitcast.core_ref, bf16[1152,128]{1,0:T(8,128)(2,1)S(1)} %edge0.1.refs_0_, bf16[3,3,3,192,192]{4,3,2,1,0:T(8,128)(2,1)S(1)} %get-tuple-element.40.refs_3_.refs_1_, f32[768,192]{1,0:T(8,128)S(1)} %get-tuple-element.45.refs_2_, ...), custom_call_target="tpu_custom_call" | custom-call | flops 509607936 | bytes 4194304 | tf_op jit(solution)/shard_map/outer1/pallas_call | solution.py:229
  31.8 3.0 %collective-permute-start.6 = (bf16[1152,128]{1,0:T(8,128)(2,1)S(1)}, bf16[1152,128]{1,0:T(8,128)(2,1)S(1)}, u32[]{:S(2)}, u32[]{:S(2)}) collective-permute-start(bf16[1152,128]{1,0:T(8,128)(2,1)S(1)} %get-tuple-element.47.refs_0_), channel_id=1, source_target_pairs={{1,2},{3,4},{5,6},{7,8},{9,10},{11,12},{13,14},{15,16},{17,18},{19... | collective-permute-start | bytes 884744 | tf_op jit(solution)/shard_map/ppermute | solution.py:355
  34.8 6.1 %local2.1 = (f32[768,192]{1,0:T(8,128)S(1)}, f32[768,192]{1,0:T(8,128)S(1)}, bf16[1152,128]{1,0:T(8,128)(2,1)S(1)}, bf16[3,3,3,192,192]{4,3,2,1,0:T(8,128)(2,1)S(1)}) custom-call(s32[1]{0:T(128)} %bitcast.core_ref, bf16[1152,128]{1,0:T(8,128)(2,1)S(1)} %get-tuple-element.47.refs_0_, bf16[1152,128]{1,0:T(8,128)(2,1)S(1)} %get-tuple-element.42.refs_1_, ...), custom_call_target="tpu_custom_call" | custom-call | flops 3057647616 | bytes 4194304 | tf_op jit(solution)/shard_map/local2/pallas_call | solution.py:229
  41.0 1.4 %collective-permute-start.8 = (bf16[1152,128]{1,0:T(8,128)(2,1)S(1)}, bf16[1152,128]{1,0:T(8,128)(2,1)S(1)}, u32[]{:S(2)}, u32[]{:S(2)}) collective-permute-start(bf16[1152,128]{1,0:T(8,128)(2,1)S(1)} %get-tuple-element.53.refs_1_), channel_id=1, source_target_pairs={{0,1},{1,0},{2,3},{3,2},{4,5},{5,4},{6,7},{7,6},{8,9},{9,8},{10,11... | collective-permute-start | bytes 884744 | tf_op jit(solution)/shard_map/ppermute | solution.py:359
  42.4 2.7 %collective-permute-done.6.refs_0_ = bf16[1152,128]{1,0:T(8,128)(2,1)S(1)} collective-permute-done((bf16[1152,128]{1,0:T(8,128)(2,1)S(1)}, bf16[1152,128]{1,0:T(8,128)(2,1)S(1)}, u32[]{:S(2)}, u32[]{:S(2)}) %collective-permute-start.6) | collective-permute-done | bytes 294944 | tf_op jit(solution)/shard_map/ppermute | solution.py:355
  45.1 1.9 %outer2.1 = (f32[768,192]{1,0:T(8,128)S(1)}, bf16[1152,128]{1,0:T(8,128)(2,1)S(1)}) custom-call(s32[1]{0:T(128)} %bitcast.core_ref, bf16[1152,128]{1,0:T(8,128)(2,1)S(1)} %collective-permute-done.6.refs_0_, bf16[3,3,3,192,192]{4,3,2,1,0:T(8,128)(2,1)S(1)} %get-tuple-element.43.refs_3_.refs_1_, f32[768,192]{1,0:T(8,128)S(1)} %get-tuple-element.48.refs_2_, ...), custom_call_target="tpu_custom_call" | custom-call | flops 1019215872 | bytes 4194304 | tf_op jit(solution)/shard_map/outer2/pallas_call | solution.py:229
  47.0 1.3 %edge2.1.refs_0_ = bf16[1152,128]{1,0:T(8,128)(2,1)S(1)} custom-call(s32[1]{0:T(128)} %bitcast.core_ref, bf16[1152,128]{1,0:T(8,128)(2,1)S(1)} %collective-permute-done.4.refs_0_, bf16[3,3,3,192,192]{4,3,2,1,0:T(8,128)(2,1)S(1)} %get-tuple-element.43.refs_3_.refs_1_, f32[768,192]{1,0:T(8,128)S(1)} %get-tuple-element.50.refs_2_, ...), custom_call_target="tpu_custom_call" | custom-call | flops 509607936 | bytes 4194304 | tf_op jit(solution)/shard_map/edge2/pallas_call | solution.py:229
  48.3 4.2 %local3.1 = (f32[768,192]{1,0:T(8,128)S(1)}, bf16[4,96,192]{2,1,0:T(8,128)(2,1)S(1)}, bf16[4,96,192]{2,1,0:T(8,128)(2,1)S(1)}) custom-call(s32[1]{0:T(128)} %bitcast.core_ref, bf16[1152,128]{1,0:T(8,128)(2,1)S(1)} %get-tuple-element.52.refs_0_, bf16[1152,128]{1,0:T(8,128)(2,1)S(1)} %get-tuple-element.53.refs_1_, ...), custom_call_target="tpu_custom_call" | custom-call | flops 2548039680 | bytes 4194304 | tf_op jit(solution)/shard_map/local3/pallas_call | solution.py:229
  52.5 1.2 %outer3.1 = (bf16[4,96,192]{2,1,0:T(8,128)(2,1)S(1)}, bf16[4,96,192]{2,1,0:T(8,128)(2,1)S(1)}) custom-call(s32[1]{0:T(128)} %bitcast.core_ref, bf16[1152,128]{1,0:T(8,128)(2,1)S(1)} %edge2.1.refs_0_, bf16[3,3,3,192,192]{4,3,2,1,0:T(8,128)(2,1)S(1)} %get-tuple-element.51.refs_3_.refs_1_, f32[768,192]{1,0:T(8,128)S(1)} %get-tuple-element.55.refs_2_, ...), custom_call_target="tpu_custom_call" | custom-call | flops 509607936 | bytes 4194304 | tf_op jit(solution)/shard_map/outer3/pallas_call | solution.py:229
  53.7 1.0 %collective-permute-start.9 = (bf16[4,96,192]{2,1,0:T(8,128)(2,1)S(1)}, bf16[4,96,192]{2,1,0:T(8,128)(2,1)S(1)}, u32[]{:S(2)}, u32[]{:S(2)}) collective-permute-start(bf16[4,96,192]{2,1,0:T(8,128)(2,1)S(1)} %get-tuple-element.59), channel_id=1, source_target_pairs={{0,1},{1,0},{2,3},{3,2},{4,5},{5,4},{6,7},{7,6},{8,9},{9,8},{10,11... | collective-permute-start | bytes 442376 | tf_op jit(solution)/shard_map/ppermute | solution.py:368
  54.7 0.1 collective-permute-start.10
  54.8 1.0 %collective-permute-done.9.refs_2_ = bf16[4,96,192]{2,1,0:T(8,128)(2,1)S(1)} collective-permute-done((bf16[4,96,192]{2,1,0:T(8,128)(2,1)S(1)}, bf16[4,96,192]{2,1,0:T(8,128)(2,1)S(1)}, u32[]{:S(2)}, u32[]{:S(2)}) %collective-permute-start.9) | collective-permute-done | bytes 147488 | tf_op jit(solution)/shard_map/ppermute | solution.py:368
  55.8 0.4 collective-permute-done.10.refs_3_
  56.1 0.9 %last.1 = bf16[4,4,96,192]{3,2,1,0:T(8,128)(2,1)} custom-call(s32[1]{0:T(128)} %bitcast.core_ref, bf16[4,96,192]{2,1,0:T(8,128)(2,1)S(1)} %get-tuple-element.57.refs_0_, bf16[4,96,192]{2,1,0:T(8,128)(2,1)S(1)} %get-tuple-element.58.refs_1_, bf16[4,96,192]{2,1,0:T(8,128)(2,1)S(1)} %collective-permute-done.9.refs_2_, ...), custom_call_target="tpu_custom_call" | custom-call | tf_op jit(solution)/shard_map/last/pallas_call | solution.py:313
  (5 shorter events, 0.0 us)
Async XLA Ops:
  1.2 2.1 %collective-permute-start = (bf16[4,2,96,192]{3,2,1,0:T(8,128)(2,1)S(1)}, bf16[4,2,96,192]{3,2,1,0:T(8,128)(2,1)S(1)}, u32[]{:S(2)}, u32[]{:S(2)}) collective-permute-start(bf16[4,2,96,192]{3,2,1,0:T(8,128)(2,1)S(1)} %get-tuple-element.61), channel_id=1, source_target_pairs={{0,1},{1,0},{2,3},{3,2},{4,5},{5,4},{6,7},{7,6},{8,9},{9,8},{10,11... | collective-permute-start | bytes 884744 | tf_op jit(solution)/shard_map/ppermute | solution.py:344
  3.8 4.1 %collective-permute-start.2 = (bf16[1152,128]{1,0:T(8,128)(2,1)S(1)}, bf16[1152,128]{1,0:T(8,128)(2,1)S(1)}, u32[]{:S(2)}, u32[]{:S(2)}) collective-permute-start(bf16[1152,128]{1,0:T(8,128)(2,1)S(1)} %get-tuple-element.34.refs_1_), channel_id=1, source_target_pairs={{0,1},{1,0},{2,3},{3,2},{4,5},{5,4},{6,7},{7,6},{8,9},{9,8},{10,11... | collective-permute-start | bytes 884744 | tf_op jit(solution)/shard_map/ppermute | solution.py:356
  4.8 13.5 %collective-permute-start.1 = (bf16[1152,128]{1,0:T(8,128)(2,1)S(1)}, bf16[1152,128]{1,0:T(8,128)(2,1)S(1)}, u32[]{:S(2)}, u32[]{:S(2)}) collective-permute-start(bf16[1152,128]{1,0:T(8,128)(2,1)S(1)} %get-tuple-element.33.refs_0_), channel_id=1, source_target_pairs={{1,2},{3,4},{5,6},{7,8},{9,10},{11,12},{13,14},{15,16},{17,18},{19... | collective-permute-start | bytes 884744 | tf_op jit(solution)/shard_map/ppermute | solution.py:355
  14.5 5.6 %collective-permute-start.3 = (bf16[1152,128]{1,0:T(8,128)(2,1)S(1)}, bf16[1152,128]{1,0:T(8,128)(2,1)S(1)}, u32[]{:S(2)}, u32[]{:S(2)}) collective-permute-start(bf16[1152,128]{1,0:T(8,128)(2,1)S(1)} %get-tuple-element.39.refs_1_), channel_id=1, source_target_pairs={{0,1},{1,0},{2,3},{3,2},{4,5},{5,4},{6,7},{7,6},{8,9},{9,8},{10,11... | collective-permute-start | bytes 884744 | tf_op jit(solution)/shard_map/ppermute | solution.py:359
  14.9 11.5 %collective-permute-start.5 = (bf16[1152,128]{1,0:T(8,128)(2,1)S(1)}, bf16[1152,128]{1,0:T(8,128)(2,1)S(1)}, u32[]{:S(2)}, u32[]{:S(2)}) collective-permute-start(bf16[1152,128]{1,0:T(8,128)(2,1)S(1)} %get-tuple-element.34.refs_1_), channel_id=1, source_target_pairs={{1,2},{3,4},{5,6},{7,8},{9,10},{11,12},{13,14},{15,16},{17,18},{19... | collective-permute-start | bytes 884744 | tf_op jit(solution)/shard_map/ppermute | solution.py:355
  24.5 10.3 %collective-permute-start.7 = (bf16[1152,128]{1,0:T(8,128)(2,1)S(1)}, bf16[1152,128]{1,0:T(8,128)(2,1)S(1)}, u32[]{:S(2)}, u32[]{:S(2)}) collective-permute-start(bf16[1152,128]{1,0:T(8,128)(2,1)S(1)} %get-tuple-element.42.refs_1_), channel_id=1, source_target_pairs={{0,1},{1,0},{2,3},{3,2},{4,5},{5,4},{6,7},{7,6},{8,9},{9,8},{10,11... | collective-permute-start | bytes 884744 | tf_op jit(solution)/shard_map/ppermute | solution.py:356
  27.7 19.3 %collective-permute-start.4 = (bf16[1152,128]{1,0:T(8,128)(2,1)S(1)}, bf16[1152,128]{1,0:T(8,128)(2,1)S(1)}, u32[]{:S(2)}, u32[]{:S(2)}) collective-permute-start(bf16[1152,128]{1,0:T(8,128)(2,1)S(1)} %get-tuple-element.42.refs_1_), channel_id=1, source_target_pairs={{1,2},{3,4},{5,6},{7,8},{9,10},{11,12},{13,14},{15,16},{17,18},{19... | collective-permute-start | bytes 884744 | tf_op jit(solution)/shard_map/ppermute | solution.py:355
  31.8 13.2 %collective-permute-start.6 = (bf16[1152,128]{1,0:T(8,128)(2,1)S(1)}, bf16[1152,128]{1,0:T(8,128)(2,1)S(1)}, u32[]{:S(2)}, u32[]{:S(2)}) collective-permute-start(bf16[1152,128]{1,0:T(8,128)(2,1)S(1)} %get-tuple-element.47.refs_0_), channel_id=1, source_target_pairs={{1,2},{3,4},{5,6},{7,8},{9,10},{11,12},{13,14},{15,16},{17,18},{19... | collective-permute-start | bytes 884744 | tf_op jit(solution)/shard_map/ppermute | solution.py:355
  41.0 7.3 %collective-permute-start.8 = (bf16[1152,128]{1,0:T(8,128)(2,1)S(1)}, bf16[1152,128]{1,0:T(8,128)(2,1)S(1)}, u32[]{:S(2)}, u32[]{:S(2)}) collective-permute-start(bf16[1152,128]{1,0:T(8,128)(2,1)S(1)} %get-tuple-element.53.refs_1_), channel_id=1, source_target_pairs={{0,1},{1,0},{2,3},{3,2},{4,5},{5,4},{6,7},{7,6},{8,9},{9,8},{10,11... | collective-permute-start | bytes 884744 | tf_op jit(solution)/shard_map/ppermute | solution.py:359
  53.7 2.1 %collective-permute-start.9 = (bf16[4,96,192]{2,1,0:T(8,128)(2,1)S(1)}, bf16[4,96,192]{2,1,0:T(8,128)(2,1)S(1)}, u32[]{:S(2)}, u32[]{:S(2)}) collective-permute-start(bf16[4,96,192]{2,1,0:T(8,128)(2,1)S(1)} %get-tuple-element.59), channel_id=1, source_target_pairs={{0,1},{1,0},{2,3},{3,2},{4,5},{5,4},{6,7},{7,6},{8,9},{9,8},{10,11... | collective-permute-start | bytes 442376 | tf_op jit(solution)/shard_map/ppermute | solution.py:368
  54.7 1.4 %collective-permute-start.10 = (bf16[4,96,192]{2,1,0:T(8,128)(2,1)S(1)}, bf16[4,96,192]{2,1,0:T(8,128)(2,1)S(1)}, u32[]{:S(2)}, u32[]{:S(2)}) collective-permute-start(bf16[4,96,192]{2,1,0:T(8,128)(2,1)S(1)} %get-tuple-element.60), channel_id=1, source_target_pairs={{0,1},{1,0},{2,3},{3,2},{4,5},{5,4},{6,7},{7,6},{8,9},{9,8},{10,11... | collective-permute-start | bytes 442376 | tf_op jit(solution)/shard_map/ppermute | solution.py:368

commit v3 on v2

--- a/solution.py
+++ b/solution.py
@@ -1,11 +1,10 @@
-import functools
-
 import jax
 import jax.numpy as jnp
 from jax import lax
 from jax.experimental import pallas as pl
 from jax.experimental.pallas import tpu as pltpu
 from jax.sharding import PartitionSpec as P
+
 
 AXES = ("rows", "tm")
 EPS = 1e-06
@@ -25,7 +24,7 @@
         self.size = width * frames
         self.rest = channels - LANES
         self.payload = self.size + self.size // 2
-        self.chunk = next(m for m in (256, 128, 64, 32, 16) if self.size % m == 0)
+        self.chunk = next(m for m in (192, 128, 64, 32, 16) if self.size % m == 0)
 
 
 def unpack(ref, start, m, sh):
@@ -146,9 +145,7 @@
     if prevs is not None:
         for j, row in enumerate(prevs):
             add(f"prev{j}", row)
-    start = weights is None
-    if not start:
-        add("w", weights)
+    add("w", weights)
     if not local:
         add("partial", partial[0])
         if ahead:
@@ -178,24 +175,17 @@
         give("packed", (sh.payload, LANES))
     if fetch:
         give("weights", kernels.shape[1:])
-    if start:
-        give("w", kernels.shape[1:])
-    scratches = scratch(len(rows), sh) + [pltpu.VMEM((n, ch), jnp.float32), pltpu.SemaphoreType.DMA((2,))]
+    scratches = scratch(len(rows), sh) + [pltpu.VMEM((n, ch), jnp.float32), pltpu.SemaphoreType.DMA(())]
 
     def kernel(core_ref, *refs):
         named = dict(zip(names + out_names, refs))
         s = refs[len(names) + len(out_names) :]
         k = len(rows)
-        if start:
-            begin = pltpu.make_async_copy(named["kernels"].at[layer], named["w"], s[2 * k + 1].at[1])
-            begin.start()
         if fetch:
-            copy = pltpu.make_async_copy(named["kernels"].at[layer + 1], named["weights"], s[2 * k + 1].at[0])
+            copy = pltpu.make_async_copy(named["kernels"].at[layer + 1], named["weights"], s[2 * k + 1])
             copy.start()
         for j in range(k):
             build(named[f"row{j}"], named.get(f"prev{j}"), s[j], s[k + j], sh)
-        if start:
-            begin.wait()
         named["act"] = s[2 * k]
         c = core_ref[0] & 1
 
@@ -226,7 +216,7 @@
             copy.wait()
 
     flops = 2 * n * 9 * ch * ch * ((5 if local else 1) + ahead)
-    got = pl.pallas_call(
+    call = pl.pallas_call(
         kernel,
         grid_spec=pltpu.PrefetchScalarGridSpec(
             num_scalar_prefetch=1,
@@ -236,64 +226,57 @@
             scratch_shapes=scratches,
         ),
         out_shape=outs,
-        name=f"{kind}{layer}",
         cost_estimate=pl.CostEstimate(flops=flops, transcendentals=0, bytes_accessed=4 << 20),
         compiler_params=pltpu.CompilerParams(vmem_limit_bytes=40 << 20),
-    )(core, *ins)
-    return dict(zip(out_names, got))
-
-
-def first_call(u, core, mine, theirs, gain, kernels, sh):
-    f, half, width, ch = mine.shape
-    fetch = kernels is not None
-    row = lambda i, c: (0, jnp.where((c[0] & 1) == 0, u, half - 1 - u), 0, 0)
-    block = (f, 1, width, ch)
-    outs = [
-        jax.ShapeDtypeStruct((sh.size, ch), jnp.bfloat16),
-        jax.ShapeDtypeStruct((sh.payload, LANES), jnp.bfloat16),
-    ] + ([jax.ShapeDtypeStruct(kernels.shape[1:], kernels.dtype)] if fetch else [])
+    )
+    return dict(zip(out_names, call(core, *ins)))
+
+
+def first_call(core, mine, theirs, gain, kernels, sh):
+    _, half, width, ch = mine.shape
     full = lambda x: pl.BlockSpec(x.shape, lambda i, c: (0,) * x.ndim)
-
-    def kernel(core_ref, own, other, gain_ref, *refs):
-        if fetch:
-            copy = pltpu.make_async_copy(refs[0].at[0], refs[3], refs[5])
-            copy.start()
-            refs = refs[1:]
-        hidden, packed, act = refs[0], refs[1], refs[-2]
+    outs = [jax.ShapeDtypeStruct((sh.size, ch), jnp.bfloat16) for _ in range(half)]
+    outs += [jax.ShapeDtypeStruct((sh.payload, LANES), jnp.bfloat16) for _ in range(half)]
+    outs.append(jax.ShapeDtypeStruct(kernels.shape[1:], kernels.dtype))
+
+    def kernel(core_ref, own, other, gain_ref, source, *refs):
+        act, sem = refs[2 * half + 1 :]
+        copy = pltpu.make_async_copy(source.at[0], refs[2 * half], sem)
+        copy.start()
         c, w, step = core_ref[0] & 1, width // 2, 16
-        for q in range(0, w, step):
-            groups = []
-            for g in range(2):
-                here = slice(g * w + q, g * w + q + step)
-                a, b = own[:, 0, here, :].astype(jnp.float32), other[:, 0, here, :].astype(jnp.float32)
-                x = jnp.concatenate([jnp.where(c == 0, a, b), jnp.where(c == 0, b, a)], axis=0)
-                groups.append(jnp.swapaxes(x, 0, 1)[:, None])
-            x = jnp.concatenate(groups, axis=1).reshape(step * sh.tile, ch)
-            rows = slice(q * sh.tile, (q + step) * sh.tile)
-            hidden[rows, :] = x.astype(hidden.dtype)
-            act[rows, :] = activate(x, gain_ref[...])
-        pack(act, packed, sh)
-        if fetch:
-            copy.wait()
+        for u in range(half):
+            row = jnp.where(c == 0, u, half - 1 - u)
+            for q in range(0, w, step):
+                groups = []
+                for g in range(2):
+                    here = slice(g * w + q, g * w + q + step)
+                    a, b = own[:, row, here, :].astype(jnp.float32), other[:, row, here, :].astype(jnp.float32)
+                    x = jnp.concatenate([jnp.where(c == 0, a, b), jnp.where(c == 0, b, a)], axis=0)
+                    groups.append(jnp.swapaxes(x, 0, 1)[:, None])
+                x = jnp.concatenate(groups, axis=1).reshape(step * sh.tile, ch)
+                rows = slice(q * sh.tile, (q + step) * sh.tile)
+                refs[u][rows, :] = x.astype(refs[u].dtype)
+                act[rows, :] = activate(x, gain_ref[...])
+            pack(act, refs[half + u], sh)
+        copy.wait()
 
     got = pl.pallas_call(
         kernel,
         grid_spec=pltpu.PrefetchScalarGridSpec(
             num_scalar_prefetch=1,
             grid=(1,),
-            in_specs=[pl.BlockSpec(block, row), pl.BlockSpec(block, row), full(gain)]
-            + ([pl.BlockSpec(memory_space=pltpu.HBM)] if fetch else []),
+            in_specs=[full(mine), full(theirs), full(gain), pl.BlockSpec(memory_space=pltpu.HBM)],
             out_specs=[full(o) for o in outs],
             scratch_shapes=[pltpu.VMEM((sh.size, ch), jnp.float32), pltpu.SemaphoreType.DMA(())],
         ),
         out_shape=outs,
-        name=f"first{u}",
+        name="first",
         compiler_params=pltpu.CompilerParams(vmem_limit_bytes=40 << 20),
-    )(core, mine, theirs, gain, *([kernels] if fetch else []))
-    return got
-
-
-def last_call(core, keeps, takens, video, sh):
+    )(core, mine, theirs, gain, kernels)
+    return list(got[:half]), list(got[half:-1]), got[-1]
+
+
+def last_call(core, keeps, takens, video):
     height = video.shape[1]
     count = len(keeps)
     full = lambda x: pl.BlockSpec(x.shape, lambda i, c: (0,) * x.ndim)
@@ -344,32 +327,33 @@
     theirs = lax.ppermute(give, AXES, chip)
     mine = lax.dynamic_slice_in_dim(video, core * half, half, axis=1)
     gain = gains[0][None, :]
-    h0, p0 = first_call(0, scalar, mine, theirs, gain, None, sh)
-    h1, p1 = first_call(1, scalar, mine, theirs, gain, None, sh)
-    weights = None
-    hidden, packed = [h0, h1], [p0, p1]
+    hidden, packed, weights = first_call(scalar, mine, theirs, gain, kernels, sh)
     for layer in range(0, kernels.shape[0], 2):
         call = lambda kind, step, rows, weights, residual, partial: conv_call(
             kind, layer + step, scalar, rows, before(rows), weights, kernels, gains, residual, partial, sh
         )
-        far = [lax.ppermute(row, AXES, outer) for row in packed]
+        far_inner = lax.ppermute(packed[1], AXES, outer)
+        far_outer = lax.ppermute(packed[0], AXES, outer)
         near = lax.ppermute(packed[1], AXES, chip)
         a = call("local", 0, packed + [near], weights, None, None)
-        weights = a.get("w", weights)
         near = lax.ppermute(a["packed"], AXES, chip)
-        b = call("outer", 0, far[:1], weights, None, [a["rest"], a["edge"]])
+        b = call("outer", 0, [far_outer], weights, None, [a["rest"], a["edge"]])
         got = call("local", 1, [b["packed"], a["packed"], near], a["weights"], hidden[1], None)
-        c = call("edge", 0, far[1:], weights, None, [b["edge"]])
+        c = call("edge", 0, [far_inner], weights, None, [b["edge"]])
         done = call("outer", 1, [c["packed"]], a["weights"], hidden[0], [got["rest"]])
         if "packed" in got:
             hidden, packed = [done["hidden"], got["hidden"]], [done["packed"], got["packed"]]
             weights = got["weights"]
 
-    takens = [lax.ppermute(part["give"], AXES, chip) for part in (done, got)]
-    return last_call(scalar, [done["keep"], got["keep"]], takens, video, sh)
+    taken = lax.ppermute(got["give"], AXES, chip)
+    takens = [lax.ppermute(done["give"], AXES, chip), taken]
+    return last_call(scalar, [done["keep"], got["keep"]], takens, video)
 
 
 def solution(mesh):
-    inner = functools.partial(body, count=mesh.shape["rows"], times=mesh.shape["tm"])
     specs = P("tm", "rows", None, None)
+
+    def inner(video, gains, kernels):
+        return body(video, gains, kernels, mesh.shape["rows"], mesh.shape["tm"])
+
     return jax.shard_map(inner, mesh=mesh, in_specs=(specs, P(), P()), out_specs=specs, check_vma=False)

time: 57.5 us -> 56.1 us (0.976)
  Pallas kernels: 32.1 us -> 29.2 us
  waiting for transfers between devices: 6.38 us -> 7.83 us
    pallas_call x10, Pallas kernels: 30.1 us -> 26.5 us  [conv_call(): return dict(zip(out_names, call(core, *ins)))]
    ppermute x6, waiting for transfers between devices: 5.86 us -> 7.31 us  [the longest x2 4.11 us: body(): far_outer = lax.ppermute(packed[0], AXES, outer)]
    pallas_call x2 -> x1, Pallas kernels: 1.07 us -> 1.76 us  [first_call(): pl.pallas_call(kernel, grid_spec=pltpu.PrefetchScalarGridSpec(num_scalar_...]
  transfers between devices with their start and end apart: 11 -> 11, of which waited for: 5 -> 5; matrix products, arithmetic and copies ran while one was open for 1% -> 2% of each run, Pallas kernels for 44% -> 38%
where the time goes in v3:
time: 56.1 us; the launch traced here: 55.8 us
  Pallas kernels  29.2 us (52%)
  starting transfers between devices  16.4 us (29%)
  waiting for transfers between devices  7.83 us (14%)
  local copies, waits for them, and re-layouts  2.02 us (4%)
    pallas_call x10, Pallas kernels, conv_call(): return dict(zip(out_names, call(core, *ins)))  26.5 us
    ppermute x2, starting transfers between devices, body(): far_inner = lax.ppermute(packed[1], AXES, outer)  6.16 us
    ppermute x2, starting transfers between devices, body(): far_outer = lax.ppermute(packed[0], AXES, outer)  6.12 us
    ppermute x2, waiting for transfers between devices, body(): far_outer = lax.ppermute(packed[0], AXES, outer)  4.11 us
    ppermute x2, waiting for transfers between devices, body(): far_inner = lax.ppermute(packed[1], AXES, outer)  1.84 us
    pallas_call x1, Pallas kernels, first_call(): pl.pallas_call(kernel, grid_spec=pltpu.PrefetchScalarGridSpec(num_scalar_...  1.76 us
    ppermute x2, starting transfers between devices, body(): near = lax.ppermute(a['packed'], AXES, chip)  1.75 us
    dynamic_slice x1, local copies, waits for them, and re-layouts, body(): give = lax.dynamic_slice_in_dim(video, (1 - core) * half, half, axis=1)  1.18 us
  transfers between devices with their start and end apart: 11, of which 5 were waited for; matrix products, arithmetic and copies ran while one was open for 2% of the time, Pallas kernels for 38%

profile of v3, /device:TPU:21, one launch (start us, length us, event | category | flops | bytes accessed | tf_op | source)
XLA Modules:
  0.0 55.8 jit_solution(3498681948925482427)
XLA Ops:
  0.0 1.2 %constant_dynamic-slice_fusion = (bf16[4,2,96,192]{3,2,1,0:T(8,128)(2,1)S(1)}, bf16[4,2,96,192]{3,2,1,0:T(8,128)(2,1)S(1)}) fusion(bf16[4,4,96,192]{3,2,1,0:T(8,128)(2,1)} %param.3, s32[]{:T(128)S(6)} %select_n.20, s32[]{:T(128)S(6)} %select_n.19), kind=kLoop, calls=%fused_computation | loop fusion | bytes 1179656 | tf_op jit(solution)/shard_map/dynamic_slice | solution.py:326
  1.2 0.7 %collective-permute-start = (bf16[4,2,96,192]{3,2,1,0:T(8,128)(2,1)S(1)}, bf16[4,2,96,192]{3,2,1,0:T(8,128)(2,1)S(1)}, u32[]{:S(2)}, u32[]{:S(2)}) collective-permute-start(bf16[4,2,96,192]{3,2,1,0:T(8,128)(2,1)S(1)} %get-tuple-element.61), channel_id=1, source_target_pairs={{0,1},{1,0},{2,3},{3,2},{4,5},{5,4},{6,7},{7,6},{8,9},{9,8},{10,11... | collective-permute-start | bytes 884744 | tf_op jit(solution)/shard_map/ppermute | solution.py:327
  1.9 0.8 %fusion = (f32[1,192]{1,0:T(1,128)S(1)}, f32[1,192]{1,0:T(1,128)S(1)}, f32[1,192]{1,0:T(1,128)S(1)}, f32[1,192]{1,0:T(1,128)S(1)}) fusion(f32[4,192]{1,0:T(4,128)} %param.4), kind=kLoop, calls=%fused_computation.2 | loop fusion | bytes 6144 | tf_op jit(solution)/shard_map/slice | solution.py:154
  2.8 0.5 collective-permute-done.other
  3.3 1.8 %first.1 = (bf16[768,192]{1,0:T(8,128)(2,1)S(1)}, bf16[768,192]{1,0:T(8,128)(2,1)S(1)}, bf16[1152,128]{1,0:T(8,128)(2,1)S(1)}, bf16[1152,128]{1,0:T(8,128)(2,1)S(1)}, bf16[3,3,3,192,192]{4,3,2,1,0:T(8,128)(2,1)S(1)}) custom-call(s32[1]{0:T(128)} %bitcast.core_ref, bf16[4,2,96,192]{3,2,1,0:T(8,128)(2,1)S(1)} %get-tuple-element.62.own, ...), custom_call_target="tpu_custom_call" | custom-call | tf_op jit(solution)/shard_map/first/pallas_call | solution.py:263
  5.0 0.4 collective-permute-start.2
  5.5 3.1 %collective-permute-start.1 = (bf16[1152,128]{1,0:T(8,128)(2,1)S(1)}, bf16[1152,128]{1,0:T(8,128)(2,1)S(1)}, u32[]{:S(2)}, u32[]{:S(2)}) collective-permute-start(bf16[1152,128]{1,0:T(8,128)(2,1)S(1)} %get-tuple-element.33.refs_0_), channel_id=1, source_target_pairs={{1,2},{3,4},{5,6},{7,8},{9,10},{11,12},{13,14},{15,16},{17,18},{19... | collective-permute-start | bytes 884744 | tf_op jit(solution)/shard_map/ppermute | solution.py:336
  8.6 0.0 collective-permute-done.2.refs_2_
  8.6 4.9 %shard_map.37 = (f32[768,192]{1,0:T(8,128)S(1)}, f32[768,192]{1,0:T(8,128)S(1)}, bf16[1152,128]{1,0:T(8,128)(2,1)S(1)}, bf16[3,3,3,192,192]{4,3,2,1,0:T(8,128)(2,1)S(1)}) custom-call(s32[1]{0:T(128)} %bitcast.core_ref, bf16[1152,128]{1,0:T(8,128)(2,1)S(1)} %get-tuple-element.33.refs_0_, bf16[1152,128]{1,0:T(8,128)(2,1)S(1)} %get-tuple-element.35.refs_1_, ...), custom_call_target="tpu_custom_call" | custom-call | flops 3057647616 | bytes 4194304 | tf_op jit(solution)/shard_map/pallas_call | solution.py:232
  13.5 0.4 collective-permute-start.3
  13.9 3.4 %collective-permute-start.5 = (bf16[1152,128]{1,0:T(8,128)(2,1)S(1)}, bf16[1152,128]{1,0:T(8,128)(2,1)S(1)}, u32[]{:S(2)}, u32[]{:S(2)}) collective-permute-start(bf16[1152,128]{1,0:T(8,128)(2,1)S(1)} %get-tuple-element.35.refs_1_), channel_id=1, source_target_pairs={{1,2},{3,4},{5,6},{7,8},{9,10},{11,12},{13,14},{15,16},{17,18},{19... | collective-permute-start | bytes 884744 | tf_op jit(solution)/shard_map/ppermute | solution.py:335
  17.3 0.0 collective-permute-done.1.refs_0_
  17.3 1.9 %shard_map.38 = (f32[768,192]{1,0:T(8,128)S(1)}, bf16[1152,128]{1,0:T(8,128)(2,1)S(1)}) custom-call(s32[1]{0:T(128)} %bitcast.core_ref, bf16[1152,128]{1,0:T(8,128)(2,1)S(1)} %collective-permute-done.1.refs_0_, bf16[3,3,3,192,192]{4,3,2,1,0:T(8,128)(2,1)S(1)} %get-tuple-element.34.refs_3_.refs_1_, f32[768,192]{1,0:T(8,128)S(1)} %get-tuple-element.36.refs_2_, ...), custom_call_target="tpu_custom_call" | custom-call | flops 1019215872 | bytes 4194304 | tf_op jit(solution)/shard_map/pallas_call | solution.py:232
  19.2 4.2 %shard_map.39 = (f32[768,192]{1,0:T(8,128)S(1)}, bf16[768,192]{1,0:T(8,128)(2,1)S(1)}, bf16[1152,128]{1,0:T(8,128)(2,1)S(1)}, bf16[3,3,3,192,192]{4,3,2,1,0:T(8,128)(2,1)S(1)}) custom-call(s32[1]{0:T(128)} %bitcast.core_ref, bf16[1152,128]{1,0:T(8,128)(2,1)S(1)} %get-tuple-element.38.refs_0_, bf16[1152,128]{1,0:T(8,128)(2,1)S(1)} %get-tuple-element.39.refs_1_, ...), custom_call_target="tpu_custom_call" | custom-call | flops 2548039680 | bytes 4194304 | tf_op jit(solution)/shard_map/pallas_call | solution.py:232
  23.4 0.1 collective-permute-start.7
  23.5 1.8 %collective-permute-done.5.refs_0_ = bf16[1152,128]{1,0:T(8,128)(2,1)S(1)} collective-permute-done((bf16[1152,128]{1,0:T(8,128)(2,1)S(1)}, bf16[1152,128]{1,0:T(8,128)(2,1)S(1)}, u32[]{:S(2)}, u32[]{:S(2)}) %collective-permute-start.5) | collective-permute-done | bytes 294944 | tf_op jit(solution)/shard_map/ppermute | solution.py:335
  25.3 1.2 %shard_map.40.refs_0_ = bf16[1152,128]{1,0:T(8,128)(2,1)S(1)} custom-call(s32[1]{0:T(128)} %bitcast.core_ref, bf16[1152,128]{1,0:T(8,128)(2,1)S(1)} %collective-permute-done.5.refs_0_, bf16[3,3,3,192,192]{4,3,2,1,0:T(8,128)(2,1)S(1)} %get-tuple-element.34.refs_3_.refs_1_, f32[768,192]{1,0:T(8,128)S(1)} %get-tuple-element.44.refs_2_, ...), custom_call_target="tpu_custom_call" | custom-call | flops 509607936 | bytes 4194304 | tf_op jit(solution)/shard_map/pallas_call | solution.py:232
  26.5 2.8 %collective-permute-start.4 = (bf16[1152,128]{1,0:T(8,128)(2,1)S(1)}, bf16[1152,128]{1,0:T(8,128)(2,1)S(1)}, u32[]{:S(2)}, u32[]{:S(2)}) collective-permute-start(bf16[1152,128]{1,0:T(8,128)(2,1)S(1)} %get-tuple-element.42.refs_1_), channel_id=1, source_target_pairs={{1,2},{3,4},{5,6},{7,8},{9,10},{11,12},{13,14},{15,16},{17,18},{19... | collective-permute-start | bytes 884744 | tf_op jit(solution)/shard_map/ppermute | solution.py:335
  29.3 1.2 %shard_map.41 = (bf16[768,192]{1,0:T(8,128)(2,1)S(1)}, bf16[1152,128]{1,0:T(8,128)(2,1)S(1)}) custom-call(s32[1]{0:T(128)} %bitcast.core_ref, bf16[1152,128]{1,0:T(8,128)(2,1)S(1)} %shard_map.40.refs_0_, bf16[3,3,3,192,192]{4,3,2,1,0:T(8,128)(2,1)S(1)} %get-tuple-element.40.refs_3_.refs_1_, f32[768,192]{1,0:T(8,128)S(1)} %get-tuple-element.45.refs_2_, ...), custom_call_target="tpu_custom_call" | custom-call | flops 509607936 | bytes 4194304 | tf_op jit(solution)/shard_map/pallas_call | solution.py:232
  30.6 3.0 %collective-permute-start.6 = (bf16[1152,128]{1,0:T(8,128)(2,1)S(1)}, bf16[1152,128]{1,0:T(8,128)(2,1)S(1)}, u32[]{:S(2)}, u32[]{:S(2)}) collective-permute-start(bf16[1152,128]{1,0:T(8,128)(2,1)S(1)} %get-tuple-element.47.refs_0_), channel_id=1, source_target_pairs={{1,2},{3,4},{5,6},{7,8},{9,10},{11,12},{13,14},{15,16},{17,18},{19... | collective-permute-start | bytes 884744 | tf_op jit(solution)/shard_map/ppermute | solution.py:336
  33.6 4.9 %shard_map.42 = (f32[768,192]{1,0:T(8,128)S(1)}, f32[768,192]{1,0:T(8,128)S(1)}, bf16[1152,128]{1,0:T(8,128)(2,1)S(1)}, bf16[3,3,3,192,192]{4,3,2,1,0:T(8,128)(2,1)S(1)}) custom-call(s32[1]{0:T(128)} %bitcast.core_ref, bf16[1152,128]{1,0:T(8,128)(2,1)S(1)} %get-tuple-element.47.refs_0_, bf16[1152,128]{1,0:T(8,128)(2,1)S(1)} %get-tuple-element.42.refs_1_, ...), custom_call_target="tpu_custom_call" | custom-call | flops 3057647616 | bytes 4194304 | tf_op jit(solution)/shard_map/pallas_call | solution.py:232
  38.5 1.4 %collective-permute-start.8 = (bf16[1152,128]{1,0:T(8,128)(2,1)S(1)}, bf16[1152,128]{1,0:T(8,128)(2,1)S(1)}, u32[]{:S(2)}, u32[]{:S(2)}) collective-permute-start(bf16[1152,128]{1,0:T(8,128)(2,1)S(1)} %get-tuple-element.53.refs_1_), channel_id=1, source_target_pairs={{0,1},{1,0},{2,3},{3,2},{4,5},{5,4},{6,7},{7,6},{8,9},{9,8},{10,11... | collective-permute-start | bytes 884744 | tf_op jit(solution)/shard_map/ppermute | solution.py:339
  39.8 4.1 %collective-permute-done.6.refs_0_ = bf16[1152,128]{1,0:T(8,128)(2,1)S(1)} collective-permute-done((bf16[1152,128]{1,0:T(8,128)(2,1)S(1)}, bf16[1152,128]{1,0:T(8,128)(2,1)S(1)}, u32[]{:S(2)}, u32[]{:S(2)}) %collective-permute-start.6) | collective-permute-done | bytes 294944 | tf_op jit(solution)/shard_map/ppermute | solution.py:336
  43.9 1.9 %shard_map.43 = (f32[768,192]{1,0:T(8,128)S(1)}, bf16[1152,128]{1,0:T(8,128)(2,1)S(1)}) custom-call(s32[1]{0:T(128)} %bitcast.core_ref, bf16[1152,128]{1,0:T(8,128)(2,1)S(1)} %collective-permute-done.6.refs_0_, bf16[3,3,3,192,192]{4,3,2,1,0:T(8,128)(2,1)S(1)} %get-tuple-element.43.refs_3_.refs_1_, f32[768,192]{1,0:T(8,128)S(1)} %get-tuple-element.48.refs_2_, ...), custom_call_target="tpu_custom_call" | custom-call | flops 1019215872 | bytes 4194304 | tf_op jit(solution)/shard_map/pallas_call | solution.py:232
  45.9 1.2 %shard_map.44.refs_0_ = bf16[1152,128]{1,0:T(8,128)(2,1)S(1)} custom-call(s32[1]{0:T(128)} %bitcast.core_ref, bf16[1152,128]{1,0:T(8,128)(2,1)S(1)} %collective-permute-done.4.refs_0_, bf16[3,3,3,192,192]{4,3,2,1,0:T(8,128)(2,1)S(1)} %get-tuple-element.43.refs_3_.refs_1_, f32[768,192]{1,0:T(8,128)S(1)} %get-tuple-element.50.refs_2_, ...), custom_call_target="tpu_custom_call" | custom-call | flops 509607936 | bytes 4194304 | tf_op jit(solution)/shard_map/pallas_call | solution.py:232
  47.1 4.0 %shard_map.45 = (f32[768,192]{1,0:T(8,128)S(1)}, bf16[4,96,192]{2,1,0:T(8,128)(2,1)S(1)}, bf16[4,96,192]{2,1,0:T(8,128)(2,1)S(1)}) custom-call(s32[1]{0:T(128)} %bitcast.core_ref, bf16[1152,128]{1,0:T(8,128)(2,1)S(1)} %get-tuple-element.52.refs_0_, bf16[1152,128]{1,0:T(8,128)(2,1)S(1)} %get-tuple-element.53.refs_1_, ...), custom_call_target="tpu_custom_call" | custom-call | flops 2548039680 | bytes 4194304 | tf_op jit(solution)/shard_map/pallas_call | solution.py:232
  51.1 1.1 %shard_map.46 = (bf16[4,96,192]{2,1,0:T(8,128)(2,1)S(1)}, bf16[4,96,192]{2,1,0:T(8,128)(2,1)S(1)}) custom-call(s32[1]{0:T(128)} %bitcast.core_ref, bf16[1152,128]{1,0:T(8,128)(2,1)S(1)} %shard_map.44.refs_0_, bf16[3,3,3,192,192]{4,3,2,1,0:T(8,128)(2,1)S(1)} %get-tuple-element.51.refs_3_.refs_1_, f32[768,192]{1,0:T(8,128)S(1)} %get-tuple-element.55.refs_2_, ...), custom_call_target="tpu_custom_call" | custom-call | flops 509607936 | bytes 4194304 | tf_op jit(solution)/shard_map/pallas_call | solution.py:232
  52.3 1.1 %collective-permute-start.9 = (bf16[4,96,192]{2,1,0:T(8,128)(2,1)S(1)}, bf16[4,96,192]{2,1,0:T(8,128)(2,1)S(1)}, u32[]{:S(2)}, u32[]{:S(2)}) collective-permute-start(bf16[4,96,192]{2,1,0:T(8,128)(2,1)S(1)} %get-tuple-element.59), channel_id=1, source_target_pairs={{0,1},{1,0},{2,3},{3,2},{4,5},{5,4},{6,7},{7,6},{8,9},{9,8},{10,11... | collective-permute-start | bytes 442376 | tf_op jit(solution)/shard_map/ppermute | solution.py:349
  53.3 0.1 collective-permute-start.10
  53.4 1.0 %collective-permute-done.9.refs_2_ = bf16[4,96,192]{2,1,0:T(8,128)(2,1)S(1)} collective-permute-done((bf16[4,96,192]{2,1,0:T(8,128)(2,1)S(1)}, bf16[4,96,192]{2,1,0:T(8,128)(2,1)S(1)}, u32[]{:S(2)}, u32[]{:S(2)}) %collective-permute-start.9) | collective-permute-done | bytes 147488 | tf_op jit(solution)/shard_map/ppermute | solution.py:349
  54.4 0.4 collective-permute-done.10.refs_3_
  54.8 0.9 %last.1 = bf16[4,4,96,192]{3,2,1,0:T(8,128)(2,1)} custom-call(s32[1]{0:T(128)} %bitcast.core_ref, bf16[4,96,192]{2,1,0:T(8,128)(2,1)S(1)} %get-tuple-element.57.refs_0_, bf16[4,96,192]{2,1,0:T(8,128)(2,1)S(1)} %get-tuple-element.58.refs_1_, bf16[4,96,192]{2,1,0:T(8,128)(2,1)S(1)} %collective-permute-done.9.refs_2_, ...), custom_call_target="tpu_custom_call" | custom-call | tf_op jit(solution)/shard_map/last/pallas_call | solution.py:296
  (4 shorter events, 0.0 us)
Async XLA Ops:
  1.2 2.1 %collective-permute-start = (bf16[4,2,96,192]{3,2,1,0:T(8,128)(2,1)S(1)}, bf16[4,2,96,192]{3,2,1,0:T(8,128)(2,1)S(1)}, u32[]{:S(2)}, u32[]{:S(2)}) collective-permute-start(bf16[4,2,96,192]{3,2,1,0:T(8,128)(2,1)S(1)} %get-tuple-element.61), channel_id=1, source_target_pairs={{0,1},{1,0},{2,3},{3,2},{4,5},{5,4},{6,7},{7,6},{8,9},{9,8},{10,11... | collective-permute-start | bytes 884744 | tf_op jit(solution)/shard_map/ppermute | solution.py:327
  5.0 3.6 %collective-permute-start.2 = (bf16[1152,128]{1,0:T(8,128)(2,1)S(1)}, bf16[1152,128]{1,0:T(8,128)(2,1)S(1)}, u32[]{:S(2)}, u32[]{:S(2)}) collective-permute-start(bf16[1152,128]{1,0:T(8,128)(2,1)S(1)} %get-tuple-element.35.refs_1_), channel_id=1, source_target_pairs={{0,1},{1,0},{2,3},{3,2},{4,5},{5,4},{6,7},{7,6},{8,9},{9,8},{10,11... | collective-permute-start | bytes 884744 | tf_op jit(solution)/shard_map/ppermute | solution.py:337
  5.5 11.8 %collective-permute-start.1 = (bf16[1152,128]{1,0:T(8,128)(2,1)S(1)}, bf16[1152,128]{1,0:T(8,128)(2,1)S(1)}, u32[]{:S(2)}, u32[]{:S(2)}) collective-permute-start(bf16[1152,128]{1,0:T(8,128)(2,1)S(1)} %get-tuple-element.33.refs_0_), channel_id=1, source_target_pairs={{1,2},{3,4},{5,6},{7,8},{9,10},{11,12},{13,14},{15,16},{17,18},{19... | collective-permute-start | bytes 884744 | tf_op jit(solution)/shard_map/ppermute | solution.py:336
  13.5 5.7 %collective-permute-start.3 = (bf16[1152,128]{1,0:T(8,128)(2,1)S(1)}, bf16[1152,128]{1,0:T(8,128)(2,1)S(1)}, u32[]{:S(2)}, u32[]{:S(2)}) collective-permute-start(bf16[1152,128]{1,0:T(8,128)(2,1)S(1)} %get-tuple-element.39.refs_1_), channel_id=1, source_target_pairs={{0,1},{1,0},{2,3},{3,2},{4,5},{5,4},{6,7},{7,6},{8,9},{9,8},{10,11... | collective-permute-start | bytes 884744 | tf_op jit(solution)/shard_map/ppermute | solution.py:339
  13.9 11.4 %collective-permute-start.5 = (bf16[1152,128]{1,0:T(8,128)(2,1)S(1)}, bf16[1152,128]{1,0:T(8,128)(2,1)S(1)}, u32[]{:S(2)}, u32[]{:S(2)}) collective-permute-start(bf16[1152,128]{1,0:T(8,128)(2,1)S(1)} %get-tuple-element.35.refs_1_), channel_id=1, source_target_pairs={{1,2},{3,4},{5,6},{7,8},{9,10},{11,12},{13,14},{15,16},{17,18},{19... | collective-permute-start | bytes 884744 | tf_op jit(solution)/shard_map/ppermute | solution.py:335
  23.4 10.2 %collective-permute-start.7 = (bf16[1152,128]{1,0:T(8,128)(2,1)S(1)}, bf16[1152,128]{1,0:T(8,128)(2,1)S(1)}, u32[]{:S(2)}, u32[]{:S(2)}) collective-permute-start(bf16[1152,128]{1,0:T(8,128)(2,1)S(1)} %get-tuple-element.42.refs_1_), channel_id=1, source_target_pairs={{0,1},{1,0},{2,3},{3,2},{4,5},{5,4},{6,7},{7,6},{8,9},{9,8},{10,11... | collective-permute-start | bytes 884744 | tf_op jit(solution)/shard_map/ppermute | solution.py:337
  26.5 19.3 %collective-permute-start.4 = (bf16[1152,128]{1,0:T(8,128)(2,1)S(1)}, bf16[1152,128]{1,0:T(8,128)(2,1)S(1)}, u32[]{:S(2)}, u32[]{:S(2)}) collective-permute-start(bf16[1152,128]{1,0:T(8,128)(2,1)S(1)} %get-tuple-element.42.refs_1_), channel_id=1, source_target_pairs={{1,2},{3,4},{5,6},{7,8},{9,10},{11,12},{13,14},{15,16},{17,18},{19... | collective-permute-start | bytes 884744 | tf_op jit(solution)/shard_map/ppermute | solution.py:335
  30.6 13.3 %collective-permute-start.6 = (bf16[1152,128]{1,0:T(8,128)(2,1)S(1)}, bf16[1152,128]{1,0:T(8,128)(2,1)S(1)}, u32[]{:S(2)}, u32[]{:S(2)}) collective-permute-start(bf16[1152,128]{1,0:T(8,128)(2,1)S(1)} %get-tuple-element.47.refs_0_), channel_id=1, source_target_pairs={{1,2},{3,4},{5,6},{7,8},{9,10},{11,12},{13,14},{15,16},{17,18},{19... | collective-permute-start | bytes 884744 | tf_op jit(solution)/shard_map/ppermute | solution.py:336
  38.5 8.6 %collective-permute-start.8 = (bf16[1152,128]{1,0:T(8,128)(2,1)S(1)}, bf16[1152,128]{1,0:T(8,128)(2,1)S(1)}, u32[]{:S(2)}, u32[]{:S(2)}) collective-permute-start(bf16[1152,128]{1,0:T(8,128)(2,1)S(1)} %get-tuple-element.53.refs_1_), channel_id=1, source_target_pairs={{0,1},{1,0},{2,3},{3,2},{4,5},{5,4},{6,7},{7,6},{8,9},{9,8},{10,11... | collective-permute-start | bytes 884744 | tf_op jit(solution)/shard_map/ppermute | solution.py:339
  52.3 2.1 %collective-permute-start.9 = (bf16[4,96,192]{2,1,0:T(8,128)(2,1)S(1)}, bf16[4,96,192]{2,1,0:T(8,128)(2,1)S(1)}, u32[]{:S(2)}, u32[]{:S(2)}) collective-permute-start(bf16[4,96,192]{2,1,0:T(8,128)(2,1)S(1)} %get-tuple-element.59), channel_id=1, source_target_pairs={{0,1},{1,0},{2,3},{3,2},{4,5},{5,4},{6,7},{7,6},{8,9},{9,8},{10,11... | collective-permute-start | bytes 442376 | tf_op jit(solution)/shard_map/ppermute | solution.py:349
  53.3 1.4 %collective-permute-start.10 = (bf16[4,96,192]{2,1,0:T(8,128)(2,1)S(1)}, bf16[4,96,192]{2,1,0:T(8,128)(2,1)S(1)}, u32[]{:S(2)}, u32[]{:S(2)}) collective-permute-start(bf16[4,96,192]{2,1,0:T(8,128)(2,1)S(1)} %get-tuple-element.60), channel_id=1, source_target_pairs={{0,1},{1,0},{2,3},{3,2},{4,5},{5,4},{6,7},{7,6},{8,9},{9,8},{10,11... | collective-permute-start | bytes 442376 | tf_op jit(solution)/shard_map/ppermute | solution.py:348

commit v4 on v3

--- a/solution.py
+++ b/solution.py
@@ -36,13 +36,17 @@
     return a.astype(jnp.float32), b.astype(jnp.float32)
 
 
-def build(ref, prev, s_ref, c_ref, sh):
+def plain(ref, start, m, sh):
+    return ref[start : start + m, :LANES], ref[start : start + m, LANES:]
+
+
+def build(ref, prev, s_ref, c_ref, sh, load=unpack):
     m = sh.tile * 8
     f, tile, n = sh.frames, sh.tile, sh.size
     edges = []
     for start in range(0, n, m):
         parts = []
-        for j, x in enumerate(unpack(ref, start, m, sh)):
+        for j, x in enumerate(load(ref, start, m, sh)):
             x3 = x.reshape(m // f, f, x.shape[-1])
             t = lax.broadcasted_iota(jnp.int32, x3.shape, 1)
             if prev is None:
@@ -232,6 +236,55 @@
     return dict(zip(out_names, call(core, *ins)))
 
 
+def beyond_call(layer, core, row, weights, gains, residual, partial, count, sh):
+    last = layer == count - 1
+    n, ch = sh.size, sh.channels
+    full = lambda x: pl.BlockSpec(x.shape, lambda i, c: (0,) * x.ndim)
+    ins = [row, *weights, *partial, residual, gains[layer][None, :]] + ([] if last else [gains[layer + 1][None, :]])
+    if last:
+        names = ["keep", "give"]
+        outs = [jax.ShapeDtypeStruct((sh.frames // 2, sh.width, ch), jnp.bfloat16) for _ in names]
+    else:
+        names = ["hidden", "packed"]
+        outs = [jax.ShapeDtypeStruct(x, jnp.bfloat16) for x in ((n, ch), (sh.payload, LANES))]
+
+    def kernel(core_ref, row_ref, w0, w1, part0, part1, residual_ref, *refs):
+        gain_refs, refs = refs[: len(ins) - 6], refs[len(ins) - 6 :]
+        s0, s1, c0, c1, act0, act1 = refs[2:]
+        c = core_ref[0] & 1
+        inside = (core_ref[0] >> 1).astype(jnp.float32)
+        index = jnp.where(c == 0, 0, 2)
+        build(row_ref, None, s0, c0, sh)
+        edge = {"act": act0, "gain": gain_refs[0]}
+        named = dict(zip(names, refs)) | {"act": act1, "gain": gain_refs[-1], "residual": residual_ref}
+        for base in range(0, n, sh.chunk):
+            acc = part0[base : base + sh.chunk, :] + taps(s0, c0, lambda dt, dq: w0[dt, index, dq], base, sh)
+            finish(acc, base, edge, sh, False, False, inside)
+        build(act0, None, s1, c1, sh, plain)
+        for base in range(0, n, sh.chunk):
+            acc = part1[base : base + sh.chunk, :] + taps(s1, c1, lambda dt, dq: w1[dt, index, dq], base, sh)
+            finish(acc, base, named, sh, True, last)
+        if last:
+            unpack_row(act1, named["keep"], named["give"], c, sh)
+        else:
+            pack(act1, named["packed"], sh)
+
+    call = pl.pallas_call(
+        kernel,
+        grid_spec=pltpu.PrefetchScalarGridSpec(
+            num_scalar_prefetch=1,
+            grid=(1,),
+            in_specs=[full(x) for x in ins],
+            out_specs=[full(o) for o in outs],
+            scratch_shapes=scratch(2, sh) + [pltpu.VMEM((n, ch), jnp.float32) for _ in range(2)],
+        ),
+        out_shape=outs,
+        cost_estimate=pl.CostEstimate(flops=36 * n * ch * ch, transcendentals=0, bytes_accessed=4 << 20),
+        compiler_params=pltpu.CompilerParams(vmem_limit_bytes=40 << 20),
+    )
+    return dict(zip(names, call(core, *ins)))
+
+
 def first_call(core, mine, theirs, gain, kernels, sh):
     _, half, width, ch = mine.shape
     full = lambda x: pl.BlockSpec(x.shape, lambda i, c: (0,) * x.ndim)
@@ -276,20 +329,20 @@
     return list(got[:half]), list(got[half:-1]), got[-1]
 
 
-def last_call(core, keeps, takens, video):
-    height = video.shape[1]
-    count = len(keeps)
+def last_call(core, parts, into, shape, dtype):
+    rows = [part[0] for part in parts]
+    height = shape[1]
     full = lambda x: pl.BlockSpec(x.shape, lambda i, c: (0,) * x.ndim)
+    hbm = pl.BlockSpec(memory_space=pltpu.HBM)
 
     def kernel(core_ref, *refs):
-        out, sems = refs[2 * count], refs[2 * count + 1]
+        out, sems = refs[-2:]
         c = core_ref[0] & 1
         copies = []
-        for j in range(count):
-            for part, upper in ((0, c == 0), (count, c != 0)):
-                row = jnp.where(upper, j, height - 1 - j)
-                copies.append(pltpu.make_async_copy(refs[part + j], out.at[:, row], sems.at[len(copies)]))
-                copies[-1].start()
+        for j, (_, place, partner) in enumerate(parts):
+            row = jnp.where(c == int(partner), place, height - 1 - place)
+            copies.append(pltpu.make_async_copy(refs[j], out.at[:, row], sems.at[j]))
+            copies[-1].start()
         for copy in copies:
             copy.wait()
 
@@ -298,14 +351,15 @@
         grid_spec=pltpu.PrefetchScalarGridSpec(
             num_scalar_prefetch=1,
             grid=(1,),
-            in_specs=[full(k) for k in keeps + takens],
-            out_specs=pl.BlockSpec(memory_space=pltpu.HBM),
-            scratch_shapes=[pltpu.SemaphoreType.DMA((2 * count,))],
+            in_specs=[full(row) for row in rows] + ([] if into is None else [hbm]),
+            out_specs=hbm,
+            scratch_shapes=[pltpu.SemaphoreType.DMA((len(rows),))],
         ),
-        out_shape=jax.ShapeDtypeStruct(video.shape, video.dtype),
+        out_shape=jax.ShapeDtypeStruct(shape, dtype),
+        input_output_aliases={} if into is None else {1 + len(rows): 0},
         name="last",
         compiler_params=pltpu.CompilerParams(vmem_limit_bytes=4 << 20),
-    )(core, *keeps, *takens)
+    )(core, *rows, *([] if into is None else [into]))
 
 
 def body(video, gains, kernels, count, times):
@@ -339,15 +393,21 @@
         near = lax.ppermute(a["packed"], AXES, chip)
         b = call("outer", 0, [far_outer], weights, None, [a["rest"], a["edge"]])
         got = call("local", 1, [b["packed"], a["packed"], near], a["weights"], hidden[1], None)
-        c = call("edge", 0, [far_inner], weights, None, [b["edge"]])
-        done = call("outer", 1, [c["packed"]], a["weights"], hidden[0], [got["rest"]])
+        if times > 2:
+            c = call("edge", 0, [far_inner], weights, None, [b["edge"]])
+            done = call("outer", 1, [c["packed"]], a["weights"], hidden[0], [got["rest"]])
+        else:
+            both, parts = [weights, a["weights"]], [b["edge"], got["rest"]]
+            done = beyond_call(layer + 1, scalar, far_inner, both, gains, hidden[0], parts, kernels.shape[0], sh)
         if "packed" in got:
             hidden, packed = [done["hidden"], got["hidden"]], [done["packed"], got["packed"]]
             weights = got["weights"]
 
     taken = lax.ppermute(got["give"], AXES, chip)
-    takens = [lax.ppermute(done["give"], AXES, chip), taken]
-    return last_call(scalar, [done["keep"], got["keep"]], takens, video)
+    late = lax.ppermute(done["give"], AXES, chip)
+    early = [(done["keep"], 0, False), (got["keep"], 1, False), (taken, 1, True)]
+    result = last_call(scalar, early, None, video.shape, video.dtype)
+    return last_call(scalar, [(late, 0, True)], result, video.shape, video.dtype)
 
 
 def solution(mesh):

time: 56.1 us -> 52.2 us (0.930)
  waiting for transfers between devices: 7.83 us -> 4.39 us
  starting transfers between devices: 16.4 us -> 15.8 us
    pallas_call x10 -> x6, Pallas kernels: 26.5 us -> 21.6 us  [conv_call(): return dict(zip(out_names, call(core, *ins)))]
    pallas_call x0 -> x2, Pallas kernels: none -> 4.5 us  [beyond_call(): return dict(zip(names, call(core, *ins)))]
    ppermute x2, waiting for transfers between devices: 4.11 us -> 0.01 us  [body(): far_outer = lax.ppermute(packed[0], AXES, outer)]
    ppermute x2, waiting for transfers between devices: 1.84 us -> 3.55 us  [body(): far_inner = lax.ppermute(packed[1], AXES, outer)]
    ppermute x1, starting transfers between devices: 0.08 us -> 1.01 us  [body(): taken = lax.ppermute(got['give'], AXES, chip)]
    ppermute x1, starting transfers between devices: 1.05 us -> 0.35 us  [body(): late = lax.ppermute(done['give'], AXES, chip)]
    ppermute x1, waiting for transfers between devices: 0.99 us -> 0.31 us  [body(): late = lax.ppermute(done['give'], AXES, chip)]
    pallas_call x1 -> x2, Pallas kernels: 0.9 us -> 1.52 us  [last_call(): pl.pallas_call(kernel, grid_spec=pltpu.PrefetchScalarGridSpec(num_scalar_...]
  transfers between devices with their start and end apart: 11 -> 11, of which waited for: 5 -> 4; matrix products, arithmetic and copies ran while one was open for 2% -> 2% of each run, Pallas kernels for 38% -> 52%
where the time goes in v4:
time: 52.2 us; the launch traced here: 51.9 us
  Pallas kernels  29.4 us (56%)
  starting transfers between devices  15.8 us (30%)
  waiting for transfers between devices  4.39 us (8%)
  local copies, waits for them, and re-layouts  2.02 us (4%)
    pallas_call x6, Pallas kernels, conv_call(): return dict(zip(out_names, call(core, *ins)))  21.6 us
    ppermute x2, starting transfers between devices, body(): far_outer = lax.ppermute(packed[0], AXES, outer)  5.92 us
    ppermute x2, starting transfers between devices, body(): far_inner = lax.ppermute(packed[1], AXES, outer)  5.85 us
    pallas_call x2, Pallas kernels, beyond_call(): return dict(zip(names, call(core, *ins)))  4.5 us
    ppermute x2, waiting for transfers between devices, body(): far_inner = lax.ppermute(packed[1], AXES, outer)  3.55 us
    pallas_call x1, Pallas kernels, first_call(): pl.pallas_call(kernel, grid_spec=pltpu.PrefetchScalarGridSpec(num_scalar_...  1.76 us
    pallas_call x2, Pallas kernels, last_call(): pl.pallas_call(kernel, grid_spec=pltpu.PrefetchScalarGridSpec(num_scalar_...  1.52 us
    ppermute x2, starting transfers between devices, body(): near = lax.ppermute(a['packed'], AXES, chip)  1.32 us
  transfers between devices with their start and end apart: 11, of which 4 were waited for; matrix products, arithmetic and copies ran while one was open for 2% of the time, Pallas kernels for 52%

profile of v4, /device:TPU:21, one launch (start us, length us, event | category | flops | bytes accessed | tf_op | source)
XLA Modules:
  0.0 51.9 jit_solution(12147732888213392147)
XLA Ops:
  0.0 1.2 %constant_dynamic-slice_fusion = (bf16[4,2,96,192]{3,2,1,0:T(8,128)(2,1)S(1)}, bf16[4,2,96,192]{3,2,1,0:T(8,128)(2,1)S(1)}) fusion(bf16[4,4,96,192]{3,2,1,0:T(8,128)(2,1)} %param.3, s32[]{:T(128)S(6)} %select_n.20, s32[]{:T(128)S(6)} %select_n.19), kind=kLoop, calls=%fused_computation | loop fusion | bytes 1179656 | tf_op jit(solution)/shard_map/dynamic_slice | solution.py:380
  1.2 0.7 %collective-permute-start = (bf16[4,2,96,192]{3,2,1,0:T(8,128)(2,1)S(1)}, bf16[4,2,96,192]{3,2,1,0:T(8,128)(2,1)S(1)}, u32[]{:S(2)}, u32[]{:S(2)}) collective-permute-start(bf16[4,2,96,192]{3,2,1,0:T(8,128)(2,1)S(1)} %get-tuple-element.61), channel_id=1, source_target_pairs={{0,1},{1,0},{2,3},{3,2},{4,5},{5,4},{6,7},{7,6},{8,9},{9,8},{10,11... | collective-permute-start | bytes 884744 | tf_op jit(solution)/shard_map/ppermute | solution.py:381
  1.9 0.8 %fusion = (f32[1,192]{1,0:T(1,128)S(1)}, f32[1,192]{1,0:T(1,128)S(1)}, f32[1,192]{1,0:T(1,128)S(1)}, f32[1,192]{1,0:T(1,128)S(1)}) fusion(f32[4,192]{1,0:T(4,128)} %param.4), kind=kLoop, calls=%fused_computation.2 | loop fusion | bytes 6144 | tf_op jit(solution)/shard_map/slice | solution.py:158
  2.8 0.5 collective-permute-done.other
  3.3 1.8 %first.1 = (bf16[768,192]{1,0:T(8,128)(2,1)S(1)}, bf16[768,192]{1,0:T(8,128)(2,1)S(1)}, bf16[1152,128]{1,0:T(8,128)(2,1)S(1)}, bf16[1152,128]{1,0:T(8,128)(2,1)S(1)}, bf16[3,3,3,192,192]{4,3,2,1,0:T(8,128)(2,1)S(1)}) custom-call(s32[1]{0:T(128)} %bitcast.core_ref, bf16[4,2,96,192]{3,2,1,0:T(8,128)(2,1)S(1)} %get-tuple-element.62.own, ...), custom_call_target="tpu_custom_call" | custom-call | tf_op jit(solution)/shard_map/first/pallas_call | solution.py:316
  5.0 0.4 collective-permute-start.2
  5.5 3.1 %collective-permute-start.1 = (bf16[1152,128]{1,0:T(8,128)(2,1)S(1)}, bf16[1152,128]{1,0:T(8,128)(2,1)S(1)}, u32[]{:S(2)}, u32[]{:S(2)}) collective-permute-start(bf16[1152,128]{1,0:T(8,128)(2,1)S(1)} %get-tuple-element.33.refs_0_), channel_id=1, source_target_pairs={{1,2},{3,4},{5,6},{7,8},{9,10},{11,12},{13,14},{15,16},{17,18},{19... | collective-permute-start | bytes 884744 | tf_op jit(solution)/shard_map/ppermute | solution.py:390
  8.6 0.0 collective-permute-done.2.refs_2_
  8.6 4.8 %shard_map.37 = (f32[768,192]{1,0:T(8,128)S(1)}, f32[768,192]{1,0:T(8,128)S(1)}, bf16[1152,128]{1,0:T(8,128)(2,1)S(1)}, bf16[3,3,3,192,192]{4,3,2,1,0:T(8,128)(2,1)S(1)}) custom-call(s32[1]{0:T(128)} %bitcast.core_ref, bf16[1152,128]{1,0:T(8,128)(2,1)S(1)} %get-tuple-element.33.refs_0_, bf16[1152,128]{1,0:T(8,128)(2,1)S(1)} %get-tuple-element.35.refs_1_, ...), custom_call_target="tpu_custom_call" | custom-call | flops 3057647616 | bytes 4194304 | tf_op jit(solution)/shard_map/pallas_call | solution.py:236
  13.5 0.4 collective-permute-start.3
  13.8 3.4 %collective-permute-start.5 = (bf16[1152,128]{1,0:T(8,128)(2,1)S(1)}, bf16[1152,128]{1,0:T(8,128)(2,1)S(1)}, u32[]{:S(2)}, u32[]{:S(2)}) collective-permute-start(bf16[1152,128]{1,0:T(8,128)(2,1)S(1)} %get-tuple-element.35.refs_1_), channel_id=1, source_target_pairs={{1,2},{3,4},{5,6},{7,8},{9,10},{11,12},{13,14},{15,16},{17,18},{19... | collective-permute-start | bytes 884744 | tf_op jit(solution)/shard_map/ppermute | solution.py:389
  17.2 1.9 %shard_map.38 = (f32[768,192]{1,0:T(8,128)S(1)}, bf16[1152,128]{1,0:T(8,128)(2,1)S(1)}) custom-call(s32[1]{0:T(128)} %bitcast.core_ref, bf16[1152,128]{1,0:T(8,128)(2,1)S(1)} %collective-permute-done.1.refs_0_, bf16[3,3,3,192,192]{4,3,2,1,0:T(8,128)(2,1)S(1)} %get-tuple-element.34.refs_3_.refs_1_.w0, f32[768,192]{1,0:T(8,128)S(1)} %get-tuple-element.36.refs_2_, ...), custom_call_target="tpu_custom_call" | custom-call | flops 1019215872 | bytes 4194304 | tf_op jit(solution)/shard_map/pallas_call | solution.py:236
  19.2 4.2 %shard_map.39 = (f32[768,192]{1,0:T(8,128)S(1)}, bf16[768,192]{1,0:T(8,128)(2,1)S(1)}, bf16[1152,128]{1,0:T(8,128)(2,1)S(1)}, bf16[3,3,3,192,192]{4,3,2,1,0:T(8,128)(2,1)S(1)}) custom-call(s32[1]{0:T(128)} %bitcast.core_ref, bf16[1152,128]{1,0:T(8,128)(2,1)S(1)} %get-tuple-element.38.refs_0_, bf16[1152,128]{1,0:T(8,128)(2,1)S(1)} %get-tuple-element.39.refs_1_, ...), custom_call_target="tpu_custom_call" | custom-call | flops 2548039680 | bytes 4194304 | tf_op jit(solution)/shard_map/pallas_call | solution.py:236
  23.3 0.1 collective-permute-start.6
  23.5 1.8 %collective-permute-done.5.row_ref = bf16[1152,128]{1,0:T(8,128)(2,1)S(1)} collective-permute-done((bf16[1152,128]{1,0:T(8,128)(2,1)S(1)}, bf16[1152,128]{1,0:T(8,128)(2,1)S(1)}, u32[]{:S(2)}, u32[]{:S(2)}) %collective-permute-start.5) | collective-permute-done | bytes 294944 | tf_op jit(solution)/shard_map/ppermute | solution.py:389
  25.3 2.3 %shard_map.40 = (bf16[768,192]{1,0:T(8,128)(2,1)S(1)}, bf16[1152,128]{1,0:T(8,128)(2,1)S(1)}) custom-call(s32[1]{0:T(128)} %bitcast.core_ref, bf16[1152,128]{1,0:T(8,128)(2,1)S(1)} %collective-permute-done.5.row_ref, bf16[3,3,3,192,192]{4,3,2,1,0:T(8,128)(2,1)S(1)} %get-tuple-element.34.refs_3_.refs_1_.w0, ...), custom_call_target="tpu_custom_call" | custom-call | flops 1019215872 | bytes 4194304 | tf_op jit(solution)/shard_map/pallas_call | solution.py:285
  27.6 2.8 %collective-permute-start.7 = (bf16[1152,128]{1,0:T(8,128)(2,1)S(1)}, bf16[1152,128]{1,0:T(8,128)(2,1)S(1)}, u32[]{:S(2)}, u32[]{:S(2)}) collective-permute-start(bf16[1152,128]{1,0:T(8,128)(2,1)S(1)} %get-tuple-element.47.refs_0_), channel_id=1, source_target_pairs={{1,2},{3,4},{5,6},{7,8},{9,10},{11,12},{13,14},{15,16},{17,18},{19... | collective-permute-start | bytes 884744 | tf_op jit(solution)/shard_map/ppermute | solution.py:390
  30.4 4.8 %shard_map.41 = (f32[768,192]{1,0:T(8,128)S(1)}, f32[768,192]{1,0:T(8,128)S(1)}, bf16[1152,128]{1,0:T(8,128)(2,1)S(1)}, bf16[3,3,3,192,192]{4,3,2,1,0:T(8,128)(2,1)S(1)}) custom-call(s32[1]{0:T(128)} %bitcast.core_ref, bf16[1152,128]{1,0:T(8,128)(2,1)S(1)} %get-tuple-element.47.refs_0_, bf16[1152,128]{1,0:T(8,128)(2,1)S(1)} %get-tuple-element.42.refs_1_, ...), custom_call_target="tpu_custom_call" | custom-call | flops 3057647616 | bytes 4194304 | tf_op jit(solution)/shard_map/pallas_call | solution.py:236
  35.3 0.9 %collective-permute-start.8 = (bf16[1152,128]{1,0:T(8,128)(2,1)S(1)}, bf16[1152,128]{1,0:T(8,128)(2,1)S(1)}, u32[]{:S(2)}, u32[]{:S(2)}) collective-permute-start(bf16[1152,128]{1,0:T(8,128)(2,1)S(1)} %get-tuple-element.53.refs_1_), channel_id=1, source_target_pairs={{0,1},{1,0},{2,3},{3,2},{4,5},{5,4},{6,7},{7,6},{8,9},{9,8},{10,11... | collective-permute-start | bytes 884744 | tf_op jit(solution)/shard_map/ppermute | solution.py:393
  36.2 2.5 %collective-permute-start.4 = (bf16[1152,128]{1,0:T(8,128)(2,1)S(1)}, bf16[1152,128]{1,0:T(8,128)(2,1)S(1)}, u32[]{:S(2)}, u32[]{:S(2)}) collective-permute-start(bf16[1152,128]{1,0:T(8,128)(2,1)S(1)} %get-tuple-element.42.refs_1_), channel_id=1, source_target_pairs={{1,2},{3,4},{5,6},{7,8},{9,10},{11,12},{13,14},{15,16},{17,18},{19... | collective-permute-start | bytes 884744 | tf_op jit(solution)/shard_map/ppermute | solution.py:389
  38.7 0.0 collective-permute-done.7.refs_0_
  38.7 1.9 %shard_map.42 = (f32[768,192]{1,0:T(8,128)S(1)}, bf16[1152,128]{1,0:T(8,128)(2,1)S(1)}) custom-call(s32[1]{0:T(128)} %bitcast.core_ref, bf16[1152,128]{1,0:T(8,128)(2,1)S(1)} %collective-permute-done.7.refs_0_, bf16[3,3,3,192,192]{4,3,2,1,0:T(8,128)(2,1)S(1)} %get-tuple-element.43.refs_3_.refs_1_.w0, f32[768,192]{1,0:T(8,128)S(1)} %get-tuple-element.49.refs_2_, ...), custom_call_target="tpu_custom_call" | custom-call | flops 1019215872 | bytes 4194304 | tf_op jit(solution)/shard_map/pallas_call | solution.py:236
  40.6 0.0 collective-permute-done.8.refs_2_
  40.6 4.0 %shard_map.43 = (f32[768,192]{1,0:T(8,128)S(1)}, bf16[4,96,192]{2,1,0:T(8,128)(2,1)S(1)}, bf16[4,96,192]{2,1,0:T(8,128)(2,1)S(1)}) custom-call(s32[1]{0:T(128)} %bitcast.core_ref, bf16[1152,128]{1,0:T(8,128)(2,1)S(1)} %get-tuple-element.52.refs_0_, bf16[1152,128]{1,0:T(8,128)(2,1)S(1)} %get-tuple-element.53.refs_1_, ...), custom_call_target="tpu_custom_call" | custom-call | flops 2548039680 | bytes 4194304 | tf_op jit(solution)/shard_map/pallas_call | solution.py:236
  44.6 1.0 %collective-permute-start.10 = (bf16[4,96,192]{2,1,0:T(8,128)(2,1)S(1)}, bf16[4,96,192]{2,1,0:T(8,128)(2,1)S(1)}, u32[]{:S(2)}, u32[]{:S(2)}) collective-permute-start(bf16[4,96,192]{2,1,0:T(8,128)(2,1)S(1)} %get-tuple-element.60), channel_id=1, source_target_pairs={{0,1},{1,0},{2,3},{3,2},{4,5},{5,4},{6,7},{7,6},{8,9},{9,8},{10,11... | collective-permute-start | bytes 442376 | tf_op jit(solution)/shard_map/ppermute | solution.py:406
  45.6 1.7 %collective-permute-done.4.row_ref = bf16[1152,128]{1,0:T(8,128)(2,1)S(1)} collective-permute-done((bf16[1152,128]{1,0:T(8,128)(2,1)S(1)}, bf16[1152,128]{1,0:T(8,128)(2,1)S(1)}, u32[]{:S(2)}, u32[]{:S(2)}) %collective-permute-start.4) | collective-permute-done | bytes 294944 | tf_op jit(solution)/shard_map/ppermute | solution.py:389
  47.3 2.2 %shard_map.44 = (bf16[4,96,192]{2,1,0:T(8,128)(2,1)S(1)}, bf16[4,96,192]{2,1,0:T(8,128)(2,1)S(1)}) custom-call(s32[1]{0:T(128)} %bitcast.core_ref, bf16[1152,128]{1,0:T(8,128)(2,1)S(1)} %collective-permute-done.4.row_ref, bf16[3,3,3,192,192]{4,3,2,1,0:T(8,128)(2,1)S(1)} %get-tuple-element.43.refs_3_.refs_1_.w0, ...), custom_call_target="tpu_custom_call" | custom-call | flops 1019215872 | bytes 4194304 | tf_op jit(solution)/shard_map/pallas_call | solution.py:285
  49.5 0.4 collective-permute-start.9
  49.9 0.0 collective-permute-done.10.refs_2_
  49.9 0.8 %last.2.refs_1_ = bf16[4,4,96,192]{3,2,1,0:T(8,128)(2,1)} custom-call(s32[1]{0:T(128)} %bitcast.core_ref, bf16[4,96,192]{2,1,0:T(8,128)(2,1)S(1)} %get-tuple-element.58.refs_0_, bf16[4,96,192]{2,1,0:T(8,128)(2,1)S(1)} %get-tuple-element.59.refs_1_, bf16[4,96,192]{2,1,0:T(8,128)(2,1)S(1)} %collective-permute-done.10.refs_2_), custom_call_target="tpu_custom_call" | custom-call | tf_op jit(solution)/shard_map/last/pallas_call | solution.py:349
  50.7 0.3 collective-permute-done.9.refs_0_
  51.0 0.7 %last.3 = bf16[4,4,96,192]{3,2,1,0:T(8,128)(2,1)} custom-call(s32[1]{0:T(128)} %bitcast.core_ref, bf16[4,96,192]{2,1,0:T(8,128)(2,1)S(1)} %collective-permute-done.9.refs_0_, bf16[4,4,96,192]{3,2,1,0:T(8,128)(2,1)} %last.2.refs_1_), custom_call_target="tpu_custom_call", output_to_operand_aliasing={{}: (2, {})} | custom-call | tf_op jit(solution)/shard_map/last/pallas_call | solution.py:349
  (3 shorter events, 0.0 us)
Async XLA Ops:
  1.2 2.1 %collective-permute-start = (bf16[4,2,96,192]{3,2,1,0:T(8,128)(2,1)S(1)}, bf16[4,2,96,192]{3,2,1,0:T(8,128)(2,1)S(1)}, u32[]{:S(2)}, u32[]{:S(2)}) collective-permute-start(bf16[4,2,96,192]{3,2,1,0:T(8,128)(2,1)S(1)} %get-tuple-element.61), channel_id=1, source_target_pairs={{0,1},{1,0},{2,3},{3,2},{4,5},{5,4},{6,7},{7,6},{8,9},{9,8},{10,11... | collective-permute-start | bytes 884744 | tf_op jit(solution)/shard_map/ppermute | solution.py:381
  5.0 3.6 %collective-permute-start.2 = (bf16[1152,128]{1,0:T(8,128)(2,1)S(1)}, bf16[1152,128]{1,0:T(8,128)(2,1)S(1)}, u32[]{:S(2)}, u32[]{:S(2)}) collective-permute-start(bf16[1152,128]{1,0:T(8,128)(2,1)S(1)} %get-tuple-element.35.refs_1_), channel_id=1, source_target_pairs={{0,1},{1,0},{2,3},{3,2},{4,5},{5,4},{6,7},{7,6},{8,9},{9,8},{10,11... | collective-permute-start | bytes 884744 | tf_op jit(solution)/shard_map/ppermute | solution.py:391
  5.5 11.7 %collective-permute-start.1 = (bf16[1152,128]{1,0:T(8,128)(2,1)S(1)}, bf16[1152,128]{1,0:T(8,128)(2,1)S(1)}, u32[]{:S(2)}, u32[]{:S(2)}) collective-permute-start(bf16[1152,128]{1,0:T(8,128)(2,1)S(1)} %get-tuple-element.33.refs_0_), channel_id=1, source_target_pairs={{1,2},{3,4},{5,6},{7,8},{9,10},{11,12},{13,14},{15,16},{17,18},{19... | collective-permute-start | bytes 884744 | tf_op jit(solution)/shard_map/ppermute | solution.py:390
  13.5 5.7 %collective-permute-start.3 = (bf16[1152,128]{1,0:T(8,128)(2,1)S(1)}, bf16[1152,128]{1,0:T(8,128)(2,1)S(1)}, u32[]{:S(2)}, u32[]{:S(2)}) collective-permute-start(bf16[1152,128]{1,0:T(8,128)(2,1)S(1)} %get-tuple-element.39.refs_1_), channel_id=1, source_target_pairs={{0,1},{1,0},{2,3},{3,2},{4,5},{5,4},{6,7},{7,6},{8,9},{9,8},{10,11... | collective-permute-start | bytes 884744 | tf_op jit(solution)/shard_map/ppermute | solution.py:393
  13.8 11.4 %collective-permute-start.5 = (bf16[1152,128]{1,0:T(8,128)(2,1)S(1)}, bf16[1152,128]{1,0:T(8,128)(2,1)S(1)}, u32[]{:S(2)}, u32[]{:S(2)}) collective-permute-start(bf16[1152,128]{1,0:T(8,128)(2,1)S(1)} %get-tuple-element.35.refs_1_), channel_id=1, source_target_pairs={{1,2},{3,4},{5,6},{7,8},{9,10},{11,12},{13,14},{15,16},{17,18},{19... | collective-permute-start | bytes 884744 | tf_op jit(solution)/shard_map/ppermute | solution.py:389
  23.3 7.1 %collective-permute-start.6 = (bf16[1152,128]{1,0:T(8,128)(2,1)S(1)}, bf16[1152,128]{1,0:T(8,128)(2,1)S(1)}, u32[]{:S(2)}, u32[]{:S(2)}) collective-permute-start(bf16[1152,128]{1,0:T(8,128)(2,1)S(1)} %get-tuple-element.42.refs_1_), channel_id=1, source_target_pairs={{0,1},{1,0},{2,3},{3,2},{4,5},{5,4},{6,7},{7,6},{8,9},{9,8},{10,11... | collective-permute-start | bytes 884744 | tf_op jit(solution)/shard_map/ppermute | solution.py:391
  27.6 11.1 %collective-permute-start.7 = (bf16[1152,128]{1,0:T(8,128)(2,1)S(1)}, bf16[1152,128]{1,0:T(8,128)(2,1)S(1)}, u32[]{:S(2)}, u32[]{:S(2)}) collective-permute-start(bf16[1152,128]{1,0:T(8,128)(2,1)S(1)} %get-tuple-element.47.refs_0_), channel_id=1, source_target_pairs={{1,2},{3,4},{5,6},{7,8},{9,10},{11,12},{13,14},{15,16},{17,18},{19... | collective-permute-start | bytes 884744 | tf_op jit(solution)/shard_map/ppermute | solution.py:390
  35.3 5.3 %collective-permute-start.8 = (bf16[1152,128]{1,0:T(8,128)(2,1)S(1)}, bf16[1152,128]{1,0:T(8,128)(2,1)S(1)}, u32[]{:S(2)}, u32[]{:S(2)}) collective-permute-start(bf16[1152,128]{1,0:T(8,128)(2,1)S(1)} %get-tuple-element.53.refs_1_), channel_id=1, source_target_pairs={{0,1},{1,0},{2,3},{3,2},{4,5},{5,4},{6,7},{7,6},{8,9},{9,8},{10,11... | collective-permute-start | bytes 884744 | tf_op jit(solution)/shard_map/ppermute | solution.py:393
  36.2 11.1 %collective-permute-start.4 = (bf16[1152,128]{1,0:T(8,128)(2,1)S(1)}, bf16[1152,128]{1,0:T(8,128)(2,1)S(1)}, u32[]{:S(2)}, u32[]{:S(2)}) collective-permute-start(bf16[1152,128]{1,0:T(8,128)(2,1)S(1)} %get-tuple-element.42.refs_1_), channel_id=1, source_target_pairs={{1,2},{3,4},{5,6},{7,8},{9,10},{11,12},{13,14},{15,16},{17,18},{19... | collective-permute-start | bytes 884744 | tf_op jit(solution)/shard_map/ppermute | solution.py:389
  44.6 5.3 %collective-permute-start.10 = (bf16[4,96,192]{2,1,0:T(8,128)(2,1)S(1)}, bf16[4,96,192]{2,1,0:T(8,128)(2,1)S(1)}, u32[]{:S(2)}, u32[]{:S(2)}) collective-permute-start(bf16[4,96,192]{2,1,0:T(8,128)(2,1)S(1)} %get-tuple-element.60), channel_id=1, source_target_pairs={{0,1},{1,0},{2,3},{3,2},{4,5},{5,4},{6,7},{7,6},{8,9},{9,8},{10,11... | collective-permute-start | bytes 442376 | tf_op jit(solution)/shard_map/ppermute | solution.py:406
  49.5 1.5 %collective-permute-start.9 = (bf16[4,96,192]{2,1,0:T(8,128)(2,1)S(1)}, bf16[4,96,192]{2,1,0:T(8,128)(2,1)S(1)}, u32[]{:S(2)}, u32[]{:S(2)}) collective-permute-start(bf16[4,96,192]{2,1,0:T(8,128)(2,1)S(1)} %get-tuple-element.57), channel_id=1, source_target_pairs={{0,1},{1,0},{2,3},{3,2},{4,5},{5,4},{6,7},{7,6},{8,9},{9,8},{10,11... | collective-permute-start | bytes 442376 | tf_op jit(solution)/shard_map/ppermute | solution.py:407
